TPU v7x, 128 devices: a whole 4x4x4 slice. The times are simulated.
128 devices in a mesh: section: 32 (over y, z, core), tensor: 4 (over x).
Axes of the slice: x: 4, y: 4, z: 4, core: 2. Of those that a mesh axis runs over, the one named last changes fastest.
Arguments:
- section_input: bfloat16 [32, 512, 4096], P('section', 'tensor'), may hold values from -6 to 6
- history: bfloat16 [32, 7, 512, 4096], P('section', None, 'tensor'), may hold values from -6 to 6
- query_weight: bfloat16 [32, 4096, 3072], P('section', None, 'tensor'), may hold values from -0.4 to 0.4
- key_weight: bfloat16 [32, 4096, 512], P('section', None, 'tensor'), may hold values from -0.4 to 0.4
- value_weight: bfloat16 [32, 4096, 512], P('section', None, 'tensor'), may hold values from -0.09375 to 0.09375
- output_weight: bfloat16 [32, 3072, 4096], P('section', 'tensor'), may hold values from -0.5 to 0.5
- mix_weights: float32 [32, 8], replicated, may hold values from 0.2 to 0.6
Outputs:
- next_input: bfloat16 [32, 512, 4096], P('section', 'tensor')
All inputs are finite; a program needn't handle non-finite values.
Results may differ from a plain program's by a relative error of at most 0.013.
The roundings to bfloat16 on the way count: a program that leaves them out, or rounds other values in their place, can miss the bound.
Values may be sent and summed in bfloat16 or wider, within the bound.
A program may use at most 128 MiB of HBM per device.

v0:
```python
import functools
import math

import jax
import jax.numpy as jnp
from jax import lax
from jax.experimental import pallas as pl
from jax.experimental.pallas import tpu as pltpu
from jax.sharding import PartitionSpec as P

HEAD_DIM = 64
DILATION_STRIDE = 4
MESH = pl.DeviceIdType.MESH
LAG = 2


def start(copy):
    copy.start()
    return copy


def tick_kernel(
    sections,
    x_hbm,
    hist_hbm,
    wq_hbm,
    wk_hbm,
    wv_hbm,
    wo_hbm,
    mix_hbm,
    out_hbm,
    x_own,
    chip_rows,
    peer_rows,
    w_all,
    w_out,
    q_all,
    k_pad,
    v_pad,
    peer_heads,
    own_heads,
    peer_keep,
    peer_give,
    peer_got,
    own_parts,
    own_got,
    x_in,
    mixed,
    hist_in,
    mix_v,
    w_sem,
    wo_sem,
    x_sem,
    mix_sem,
    hist_s,
    hist_r,
    sib_s,
    sib_r,
    gx_s,
    gx_r,
    fw_s,
    fw_r,
    ps_s,
    ps_r,
    os_s,
    os_r,
    xs_s,
    xs_r,
    out_s,
    out_r,
    block_in,
    store_sem,
):
    section = lax.axis_index("section")
    me = lax.axis_index("tensor")
    hi, lo = me // 2, me % 2
    sibling = hi * 2 + (1 - lo)
    peer = (1 - hi) * 2 + lo
    rows, width = x_own.shape
    slots = hist_in.shape[0]
    piece = rows // 2
    q_tiles = w_all.shape[0] - 1
    tile = w_all.shape[2]
    half = tile // 2
    col_chunks, _, cols = w_out.shape
    side = col_chunks // 2
    nxt = lax.rem(section + 1, sections)
    prv = lax.rem(section + sections - 1, sections)

    load_x = start(pltpu.make_async_copy(x_hbm.at[0], x_own, x_sem))
    barrier = pltpu.get_barrier_semaphore()
    for other in (sibling, peer, (1 - hi) * 2 + (1 - lo)):
        pl.semaphore_signal(barrier, inc=1, device_id={"tensor": other}, device_id_type=MESH)
    for other in (nxt, prv):
        pl.semaphore_signal(barrier, inc=1, device_id={"section": other}, device_id_type=MESH)
    expected = jnp.int32(5)
    for k in range(1, slots + 1):
        step = DILATION_STRIDE * k
        forward, backward = section + step < sections, prv >= step

        @pl.when(forward)
        def _():
            pl.semaphore_signal(
                barrier,
                inc=1,
                device_id={"section": lax.rem(section + step + 1, sections)},
                device_id_type=MESH,
            )

        @pl.when(backward)
        def _():
            pl.semaphore_signal(
                barrier, inc=1, device_id={"section": prv - step}, device_id_type=MESH
            )

        expected = expected + forward.astype(jnp.int32) + backward.astype(jnp.int32)

    loads = []
    for j in range(q_tiles):
        loads.append(
            pltpu.make_async_copy(
                wq_hbm.at[0, :, pl.ds(j * tile, tile)], w_all.at[j], w_sem.at[j]
            )
        )
    loads.append(
        pltpu.make_async_copy(
            wk_hbm.at[0], w_all.at[q_tiles, :, pl.ds(0, half)], w_sem.at[q_tiles]
        )
    )
    loads.append(
        pltpu.make_async_copy(
            wv_hbm.at[0], w_all.at[q_tiles, :, pl.ds(half, half)], w_sem.at[q_tiles + 1]
        )
    )
    load_x.wait()
    for copy in loads:
        copy.start()
    load_mix = start(pltpu.make_async_copy(mix_hbm, mix_v, mix_sem))
    mine = pl.multiple_of(lo * rows, rows)

    def norm_rows(i, carry):
        at = pl.multiple_of(i * 16, 16)
        values = x_own[pl.ds(at, 16), :].astype(jnp.float32)
        inv = lax.rsqrt(jnp.mean(values * values, axis=-1, keepdims=True) + 1e-05)
        chip_rows[pl.ds(pl.multiple_of(mine + at, 16), 16), :] = (values * inv).astype(jnp.bfloat16)
        return carry

    lax.fori_loop(0, rows // 16, norm_rows, 0)
    pl.semaphore_wait(barrier, expected)

    def gather_copy(j):
        return pltpu.make_async_remote_copy(
            src_ref=chip_rows.at[pl.ds(pl.multiple_of(j * rows + lo * piece, piece), piece)],
            dst_ref=peer_rows.at[j, pl.ds(pl.multiple_of(lo * piece, piece), piece)],
            send_sem=gx_s.at[j],
            recv_sem=gx_r.at[j],
            device_id={"tensor": peer},
            device_id_type=MESH,
        )

    def forward_copy(j):
        place = peer_rows.at[j, pl.ds(pl.multiple_of(lo * piece, piece), piece)]
        return pltpu.make_async_remote_copy(
            src_ref=place,
            dst_ref=place,
            send_sem=fw_s.at[j],
            recv_sem=fw_r.at[j],
            device_id={"tensor": sibling},
            device_id_type=MESH,
        )

    def sibling_copy(i):
        which = 1 - lo if i == 0 else lo
        place = chip_rows.at[pl.ds(pl.multiple_of(mine + which * piece, piece), piece)]
        return pltpu.make_async_remote_copy(
            src_ref=place,
            dst_ref=place,
            send_sem=sib_s.at[i],
            recv_sem=sib_r.at[i],
            device_id={"tensor": sibling},
            device_id_type=MESH,
        )

    @pl.when(lo == 0)
    def _():
        gather_copy(0).start()

    for i in range(2):
        sibling_copy(i).start()
    sibling_copy(0).wait_recv()

    @pl.when(lo == 1)
    def _():
        gather_copy(0).start()

    gather_copy(1).start()

    def hist_copy(k):
        return pltpu.make_async_remote_copy(
            src_ref=hist_hbm.at[0, k - 1],
            dst_ref=hist_in.at[k - 1],
            send_sem=hist_s.at[k - 1],
            recv_sem=hist_r.at[k - 1],
            device_id={"section": lax.rem(section + DILATION_STRIDE * k + 1, sections)},
            device_id_type=MESH,
        )

    for k in range(1, slots + 1):
        step = DILATION_STRIDE * k

        @pl.when(section + step < sections)
        def _():
            hist_copy(k).start()

        @pl.when(prv < step)
        def _():
            hist_in[k - 1] = jnp.zeros((rows, width), hist_in.dtype)

    out_loads = []
    for c in range(col_chunks):
        out_loads.append(
            start(
                pltpu.make_async_copy(
                    wo_hbm.at[0, :, pl.ds(c * cols, cols)], w_out.at[c], wo_sem.at[c]
                )
            )
        )

    scale = 1.0 / math.sqrt(HEAD_DIM)

    def project_query(rows_ref, target):
        size = rows_ref.shape[0]
        where = pl.ds(pl.multiple_of(target, size), size)

        def q_tile(j, carry):
            acc = jnp.dot(rows_ref[...], w_all[j], preferred_element_type=jnp.float32)
            acc = acc.astype(jnp.bfloat16) * jnp.bfloat16(scale)
            q_all[2 * j, where, :] = acc[:, :half]
            q_all[2 * j + 1, where, :] = acc[:, half:]
            return carry

        lax.fori_loop(0, q_tiles, q_tile, 0)

    def project_key_value(rows_ref, target):
        size = rows_ref.shape[0]
        where = pl.ds(pl.multiple_of(target, size), size)
        acc = jnp.dot(rows_ref[...], w_all[q_tiles], preferred_element_type=jnp.float32)
        acc = acc.astype(jnp.bfloat16).astype(jnp.float32)
        for part, padded in ((acc[:, :half], k_pad), (acc[:, half:], v_pad)):
            lane = lax.broadcasted_iota(jnp.int32, part.shape, 1)
            turned = pltpu.roll(part, HEAD_DIM, 1)
            low = lane < HEAD_DIM
            zero = jnp.zeros_like(part)
            forms = (
                jnp.where(low, part, zero),
                jnp.where(low, zero, turned),
                jnp.where(low, turned, zero),
                jnp.where(low, zero, part),
            )
            for f, form in enumerate(forms):
                padded[f, where, :] = form.astype(jnp.bfloat16)

    pairs = q_all.shape[0]
    pairs_per_kv = pairs // (half // HEAD_DIM)

    def attend(heads_ref, first, size, keys):
        def pair(p, carry):
            query = q_all[p, first : first + size, :]
            row_at = first + lax.broadcasted_iota(jnp.int32, (size, keys), 0)
            key_at = lax.broadcasted_iota(jnp.int32, (size, keys), 1)
            seen = row_at >= key_at
            kv = p // pairs_per_kv
            total = None
            for which in range(2):
                scores = lax.dot_general(
                    query,
                    k_pad[kv * 2 + which, :keys, :],
                    (((1,), (1,)), ((), ())),
                    preferred_element_type=jnp.float32,
                )
                scores = jnp.where(seen, scores, -1e30)
                top = jnp.max(scores, axis=-1, keepdims=True)
                weights = jnp.exp(scores - top)
                weights = weights * (1.0 / jnp.sum(weights, axis=-1, keepdims=True))
                term = jnp.dot(
                    weights.astype(jnp.bfloat16),
                    v_pad[kv * 2 + which, :keys, :],
                    preferred_element_type=jnp.float32,
                )
                total = term if total is None else total + term
            heads_ref[:, pl.ds(pl.multiple_of(p * half, half), half)] = total.astype(jnp.bfloat16)
            return carry

        lax.fori_loop(0, pairs, pair, 0)

    def give_copy(j, i):
        return pltpu.make_async_remote_copy(
            src_ref=peer_give.at[j, i],
            dst_ref=peer_got.at[j, i],
            send_sem=ps_s.at[j, i],
            recv_sem=ps_r.at[j, i],
            device_id={"tensor": sibling},
            device_id_type=MESH,
        )

    def cross_copy(j, i):
        return pltpu.make_async_remote_copy(
            src_ref=peer_keep.at[j, i],
            dst_ref=x_in.at[lo * side + i],
            send_sem=xs_s.at[j, i],
            recv_sem=xs_r.at[lo * side + i],
            device_id={"tensor": (1 - hi) * 2 + j},
            device_id_type=MESH,
        )

    def cross_arrival(c):
        return pltpu.make_async_remote_copy(
            src_ref=x_in.at[c],
            dst_ref=x_in.at[c],
            send_sem=xs_s.at[0, 0],
            recv_sem=xs_r.at[c],
            device_id={"tensor": peer},
            device_id_type=MESH,
        )

    def peer_output(j):
        def part(c):
            acc = jnp.dot(peer_heads[j], w_out[c], preferred_element_type=jnp.float32)
            return acc.astype(jnp.bfloat16)

        def step(i, carry):
            @pl.when(i < side)
            def _():
                peer_give[j, i] = part((1 - lo) * side + i)
                peer_keep[j, i] = part(lo * side + i)
                give_copy(j, i).start()

            @pl.when(i >= LAG)
            def _():
                at = i - LAG
                give_copy(j, at).wait_recv()
                total = peer_keep[j, at].astype(jnp.float32) + peer_got[j, at].astype(jnp.float32)
                peer_keep[j, at] = total.astype(jnp.bfloat16)
                cross_copy(j, at).start()

            return carry

        lax.fori_loop(0, side + LAG, step, 0)

    def own_copy(c):
        return pltpu.make_async_remote_copy(
            src_ref=own_parts.at[c, 1 - lo],
            dst_ref=own_got.at[c],
            send_sem=os_s.at[c],
            recv_sem=os_r.at[c],
            device_id={"tensor": sibling},
            device_id_type=MESH,
        )

    def own_part(c):
        acc = jnp.dot(own_heads[...], w_out[c], preferred_element_type=jnp.float32)
        acc = acc.astype(jnp.bfloat16)
        own_parts[c, 0] = acc[:rows]
        own_parts[c, 1] = acc[rows:]
        own_copy(c).start()

    def out_copy(c):
        return pltpu.make_async_remote_copy(
            src_ref=mixed.at[c],
            dst_ref=block_in.at[c],
            send_sem=out_s.at[c],
            recv_sem=out_r.at[c],
            device_id={"section": nxt},
            device_id_type=MESH,
        )

    for copy in loads:
        copy.wait()
    sibling_copy(1).wait_recv()
    project_key_value(chip_rows, hi * 2 * rows)
    project_query(chip_rows, hi * 2 * rows)
    for copy in out_loads:
        copy.wait()
    load_mix.wait()

    @pl.when(hi == 0)
    def _():
        attend(own_heads, 0, 2 * rows, 2 * rows)

        def own_step(c, carry):
            own_part(c)
            return carry

        lax.fori_loop(0, col_chunks, own_step, 0)

    def final_chunk(c):
        own_copy(c).wait_recv()
        total = own_parts[c, lo].astype(jnp.float32) + own_got[c].astype(jnp.float32)
        where = pl.ds(pl.multiple_of(c * cols, cols), cols)
        cross_arrival(c).wait_recv()
        total = total + x_in[c].astype(jnp.float32)
        block = (x_own[:, where].astype(jnp.float32) + total).astype(jnp.bfloat16)
        mixed[c] = block
        out_copy(c).start()

    def column(i):
        return (i % 2) * side + i // 2

    def finish():
        def final_step(i, carry):
            final_chunk(column(i))
            return carry

        lax.fori_loop(0, col_chunks, final_step, 0)

    def peer_queries(j):
        project_query(peer_rows.at[j], ((1 - hi) * 2 + j) * rows)

        @pl.when(hi == 0)
        def _():
            attend(peer_heads.at[j], (2 + j) * rows, rows, (3 + j) * rows)

        @pl.when(hi == 1)
        def _():
            attend(peer_heads.at[j], j * rows, rows, (1 + j) * rows)

        peer_output(j)

    for j in range(2):
        gather_copy(j).wait_recv()
        forward_copy(j).start()
        forward_copy(j).wait_recv()
        project_key_value(peer_rows.at[j], ((1 - hi) * 2 + j) * rows)
        if j == 0:
            peer_queries(j)

    @pl.when(hi == 1)
    def _():
        attend(own_heads, 2 * rows, 2 * rows, 4 * rows)

        def own_step(i, carry):
            own_part(column(i))

            @pl.when((lo == 0) & (i >= LAG))
            def _():
                final_chunk(column(i - LAG))

            return carry

        lax.fori_loop(0, col_chunks, own_step, 0)

        @pl.when(lo == 0)
        def _():
            for i in range(col_chunks - LAG, col_chunks):
                final_chunk(column(i))

    peer_queries(1)

    @pl.when((hi == 0) | (lo == 1))
    def _():
        finish()

    for k in range(1, slots + 1):

        @pl.when(prv >= DILATION_STRIDE * k)
        def _():
            hist_copy(k).wait_recv()

    def store_copy(c):
        return pltpu.make_async_copy(
            block_in.at[c],
            out_hbm.at[0, :, pl.ds(pl.multiple_of(c * cols, cols), cols)],
            store_sem.at[c],
        )

    def mix_step(i, carry):
        c = column(i)
        out_copy(c).wait_recv()
        where = pl.ds(pl.multiple_of(c * cols, cols), cols)
        factors = mix_v[pl.ds(prv, 1), :]
        value = factors[:, 0:1] * block_in[c].astype(jnp.float32)
        for k in range(1, slots + 1):
            past = hist_in[k - 1, :, where].astype(jnp.float32)
            value = value + factors[:, k : k + 1] * past
        block_in[c] = value.astype(jnp.bfloat16)
        store_copy(c).start()
        return carry

    lax.fori_loop(0, col_chunks, mix_step, 0)

    for i in range(2):
        sibling_copy(i).wait_send()
        gather_copy(i).wait_send()
        forward_copy(i).wait_send()
    for k in range(1, slots + 1):

        @pl.when(section + DILATION_STRIDE * k < sections)
        def _():
            hist_copy(k).wait_send()

    def drain(c, carry):
        j, i = c // side, c % side
        give_copy(j, i).wait_send()
        cross_copy(j, i).wait_send()
        own_copy(c).wait_send()
        out_copy(c).wait_send()
        store_copy(c).wait()
        return carry

    lax.fori_loop(0, col_chunks, drain, 0)


def solution(mesh):
    sections, tensor = mesh.shape["section"], mesh.shape["tensor"]
    assert tensor == 4
    col_chunks = 8

    def on_device(x, history, wq, wk, wv, wo, mix_weights):
        rows, width = x.shape[1:]
        slots = history.shape[1]
        q_width, kv_width = wq.shape[2], wk.shape[2]
        seq = rows * tensor
        tile = 2 * kv_width
        q_tiles = q_width // tile
        cols = width // col_chunks
        bf16 = jnp.bfloat16
        dma = pltpu.SemaphoreType.DMA
        hbm = pl.BlockSpec(memory_space=pl.ANY)
        return pl.pallas_call(
            functools.partial(tick_kernel, sections),
            out_shape=jax.ShapeDtypeStruct(x.shape, bf16),
            in_specs=[hbm] * 7,
            out_specs=hbm,
            scratch_shapes=[
                pltpu.VMEM((rows, width), bf16),
                pltpu.VMEM((2 * rows, width), bf16),
                pltpu.VMEM((2, rows, width), bf16),
                pltpu.VMEM((q_tiles + 1, width, tile), bf16),
                pltpu.VMEM((col_chunks, q_width, cols), bf16),
                pltpu.VMEM((2 * q_tiles, seq, kv_width), bf16),
                pltpu.VMEM((4, seq, kv_width), bf16),
                pltpu.VMEM((4, seq, kv_width), bf16),
                pltpu.VMEM((2, rows, q_width), bf16),
                pltpu.VMEM((2 * rows, q_width), bf16),
                pltpu.VMEM((2, col_chunks // 2, rows, cols), bf16),
                pltpu.VMEM((2, col_chunks // 2, rows, cols), bf16),
                pltpu.VMEM((2, col_chunks // 2, rows, cols), bf16),
                pltpu.VMEM((col_chunks, 2, rows, cols), bf16),
                pltpu.VMEM((col_chunks, rows, cols), bf16),
                pltpu.VMEM((col_chunks, rows, cols), bf16),
                pltpu.VMEM((col_chunks, rows, cols), bf16),
                pltpu.VMEM((slots, rows, width), bf16),
                pltpu.VMEM(mix_weights.shape, mix_weights.dtype),
                dma((q_tiles + 2,)),
                dma((col_chunks,)),
                dma,
                dma,
                dma((slots,)),
                dma((slots,)),
                dma((2,)),
                dma((2,)),
                dma((2,)),
                dma((2,)),
                dma((2,)),
                dma((2,)),
                dma((2, col_chunks // 2)),
                dma((2, col_chunks // 2)),
                dma((col_chunks,)),
                dma((col_chunks,)),
                dma((2, col_chunks // 2)),
                dma((col_chunks,)),
                dma((col_chunks,)),
                dma((col_chunks,)),
                pltpu.VMEM((col_chunks, rows, cols), bf16),
                dma((col_chunks,)),
            ],
            compiler_params=pltpu.CompilerParams(
                collective_id=0, has_side_effects=True, vmem_limit_bytes=60 * 1024 * 1024
            ),
        )(x, history, wq, wk, wv, wo, mix_weights)

    placed = (
        P("section", "tensor", None),
        P("section", None, "tensor", None),
        P("section", None, "tensor"),
        P("section", None, "tensor"),
        P("section", None, "tensor"),
        P("section", "tensor", None),
        P(),
    )
    return jax.shard_map(
        on_device,
        mesh=mesh,
        in_specs=placed,
        out_specs=P("section", "tensor", None),
        check_vma=False,
    )
```

profile of v0, /device:TPU:10, one launch (start us, length us, event | category | flops | bytes accessed | tf_op | source)
XLA Modules:
  0.0 172.5 jit_solution(13144816654101037918)
XLA Ops:
  0.0 1.4 copy.8.mix_hbm
  1.4 168.9 %shard_map.73 = bf16[1,128,4096]{2,1,0:T(8,128)(2,1)} custom-call(bf16[1,128,4096]{2,1,0:T(8,128)(2,1)} %x_hbm.1, bf16[1,7,128,4096]{3,2,1,0:T(8,128)(2,1)} %hist_hbm.1, bf16[1,4096,768]{2,1,0:T(8,128)(2,1)} %wq_hbm.1, bf16[1,4096,128]{2,1,0:T(8,128)(2,1)} %wk_hbm.1, bf16[1,4096,128]{2,1,0:T(8,128)(2,1)} %wv_hbm.1, bf16[1,768,4096]{2,1,0:T(8,128)(2,1)} %wo_hbm.1, ...), custom_call_target="tpu_custom_call" | custom-call | tf_op jit(solution)/shard_map/pallas_call | solution.py:529
  170.2 2.3 %copy.10 = bf16[1,128,4096]{2,1,0:T(8,128)(2,1)} copy(bf16[1,128,4096]{2,1,0:T(8,128)(2,1)} %shard_map.73) | data formatting | bytes 2097152
where the time goes:
time: 173 us
  Pallas kernels  169 us (98%)
  local copies, waits for them, and re-layouts  3.65 us (2%)
    pallas_call x1, Pallas kernels, on_device(): pl.pallas_call(functools.partial(tick_kernel, sections), out_shape=jax.Sh...  169 us
    unnamed x2, local copies, waits for them, and re-layouts  3.65 us

commit v1 on v0

v1 whole, which is shorter than its diff:
```python
import functools
import math

import jax
import jax.numpy as jnp
from jax import lax
from jax.experimental import pallas as pl
from jax.experimental.pallas import tpu as pltpu
from jax.sharding import PartitionSpec as P

HEAD_DIM = 64
DILATION_STRIDE = 4
MESH = pl.DeviceIdType.MESH
PIECES = 4


def start(copy):
    copy.start()
    return copy


def tick_kernel(
    sections,
    x_hbm,
    hist_hbm,
    wq_hbm,
    wk_hbm,
    wv_hbm,
    wo_hbm,
    mix_hbm,
    out_hbm,
    x_own,
    rows_all,
    w_all,
    w_out,
    q_all,
    k_pad,
    v_pad,
    heads,
    far_send,
    relay_in,
    near_send,
    final_in,
    own_part,
    mixed,
    block_in,
    hist_in,
    mix_v,
    w_sem,
    wo_sem,
    x_sem,
    mix_sem,
    hist_s,
    hist_r,
    ag_s,
    ag_r,
    fw_s,
    fw_r,
    far_s,
    far_r,
    near_s,
    near_r,
    out_s,
    out_r,
    store_sem,
):
    section = lax.axis_index("section")
    me = lax.axis_index("tensor")
    right, left, far = lax.rem(me + 1, 4), lax.rem(me + 3, 4), lax.rem(me + 2, 4)
    to = (right, left)
    source = (left, right)
    rows, width = x_own.shape
    slots = hist_in.shape[0]
    piece = rows // PIECES
    q_tiles = w_all.shape[0] - 1
    tile = w_all.shape[2]
    half = tile // 2
    col_chunks, _, cols = w_out.shape
    side = col_chunks // 2
    nxt = lax.rem(section + 1, sections)
    prv = lax.rem(section + sections - 1, sections)

    load_x = start(pltpu.make_async_copy(x_hbm.at[0], x_own, x_sem))
    barrier = pltpu.get_barrier_semaphore()
    for other in to:
        pl.semaphore_signal(barrier, inc=1, device_id={"tensor": other}, device_id_type=MESH)
    for other in (nxt, prv):
        pl.semaphore_signal(barrier, inc=1, device_id={"section": other}, device_id_type=MESH)
    expected = jnp.int32(4)
    for k in range(1, slots + 1):
        step = DILATION_STRIDE * k
        forward, backward = section + step < sections, prv >= step

        @pl.when(forward)
        def _():
            pl.semaphore_signal(
                barrier,
                inc=1,
                device_id={"section": lax.rem(section + step + 1, sections)},
                device_id_type=MESH,
            )

        @pl.when(backward)
        def _():
            pl.semaphore_signal(
                barrier, inc=1, device_id={"section": prv - step}, device_id_type=MESH
            )

        expected = expected + forward.astype(jnp.int32) + backward.astype(jnp.int32)

    loads = []
    for j in range(q_tiles):
        loads.append(
            pltpu.make_async_copy(
                wq_hbm.at[0, :, pl.ds(j * tile, tile)], w_all.at[j], w_sem.at[j]
            )
        )
    loads.append(
        pltpu.make_async_copy(
            wk_hbm.at[0], w_all.at[q_tiles, :, pl.ds(0, half)], w_sem.at[q_tiles]
        )
    )
    loads.append(
        pltpu.make_async_copy(
            wv_hbm.at[0], w_all.at[q_tiles, :, pl.ds(half, half)], w_sem.at[q_tiles + 1]
        )
    )
    load_x.wait()
    for copy in loads:
        copy.start()
    load_mix = start(pltpu.make_async_copy(mix_hbm, mix_v, mix_sem))

    def norm_rows(i, carry):
        at = pl.multiple_of(i * 16, 16)
        values = x_own[pl.ds(at, 16), :].astype(jnp.float32)
        inv = lax.rsqrt(jnp.mean(values * values, axis=-1, keepdims=True) + 1e-05)
        rows_all[me, pl.ds(at, 16), :] = (values * inv).astype(jnp.bfloat16)
        return carry

    lax.fori_loop(0, rows // 16, norm_rows, 0)
    pl.semaphore_wait(barrier, expected)

    def own_copy(way, p):
        place = rows_all.at[me, pl.ds(p * piece, piece)]
        return pltpu.make_async_remote_copy(
            src_ref=place,
            dst_ref=place,
            send_sem=ag_s.at[way, p],
            recv_sem=ag_r.at[way, p],
            device_id={"tensor": to[way]},
            device_id_type=MESH,
        )

    def pass_copy(p):
        way = 0 if p < PIECES // 2 else 1
        place = rows_all.at[source[way], pl.ds(p * piece, piece)]
        return pltpu.make_async_remote_copy(
            src_ref=place,
            dst_ref=place,
            send_sem=fw_s.at[p],
            recv_sem=fw_r.at[p],
            device_id={"tensor": to[way]},
            device_id_type=MESH,
        )

    for p in range(PIECES):
        own_copy(0, p).start()
        own_copy(1, PIECES - 1 - p).start()

    def hist_copy(k):
        return pltpu.make_async_remote_copy(
            src_ref=hist_hbm.at[0, k - 1],
            dst_ref=hist_in.at[k - 1],
            send_sem=hist_s.at[k - 1],
            recv_sem=hist_r.at[k - 1],
            device_id={"section": lax.rem(section + DILATION_STRIDE * k + 1, sections)},
            device_id_type=MESH,
        )

    for k in range(1, slots + 1):
        step = DILATION_STRIDE * k

        @pl.when(section + step < sections)
        def _():
            hist_copy(k).start()

        @pl.when(prv < step)
        def _():
            hist_in[k - 1] = jnp.zeros((rows, width), hist_in.dtype)

    out_loads = []
    for c in range(col_chunks):
        out_loads.append(
            start(
                pltpu.make_async_copy(
                    wo_hbm.at[0, :, pl.ds(c * cols, cols)], w_out.at[c], wo_sem.at[c]
                )
            )
        )

    scale = 1.0 / math.sqrt(HEAD_DIM)

    def project(block):
        where = pl.ds(pl.multiple_of(block * rows, rows), rows)

        def q_tile(j, carry):
            acc = jnp.dot(rows_all[block], w_all[j], preferred_element_type=jnp.float32)
            acc = acc.astype(jnp.bfloat16) * jnp.bfloat16(scale)
            q_all[2 * j, where, :] = acc[:, :half]
            q_all[2 * j + 1, where, :] = acc[:, half:]
            return carry

        lax.fori_loop(0, q_tiles, q_tile, 0)
        acc = jnp.dot(rows_all[block], w_all[q_tiles], preferred_element_type=jnp.float32)
        acc = acc.astype(jnp.bfloat16).astype(jnp.float32)
        for part, padded in ((acc[:, :half], k_pad), (acc[:, half:], v_pad)):
            lane = lax.broadcasted_iota(jnp.int32, part.shape, 1)
            turned = pltpu.roll(part, HEAD_DIM, 1)
            low = lane < HEAD_DIM
            zero = jnp.zeros_like(part)
            forms = (
                jnp.where(low, part, zero),
                jnp.where(low, zero, turned),
                jnp.where(low, turned, zero),
                jnp.where(low, zero, part),
            )
            for f, form in enumerate(forms):
                padded[f, where, :] = form.astype(jnp.bfloat16)

    pairs = q_all.shape[0]
    pairs_per_kv = pairs // (half // HEAD_DIM)

    def attend(block, wanted):
        for b in range(4):
            keys = (b + 1) * rows

            @pl.when(wanted & (block == b))
            def _():
                def pair(p, carry):
                    query = q_all[p, b * rows : (b + 1) * rows, :]
                    row_at = b * rows + lax.broadcasted_iota(jnp.int32, (rows, keys), 0)
                    key_at = lax.broadcasted_iota(jnp.int32, (rows, keys), 1)
                    seen = row_at >= key_at
                    kv = p // pairs_per_kv
                    total = None
                    for which in range(2):
                        scores = lax.dot_general(
                            query,
                            k_pad[kv * 2 + which, :keys, :],
                            (((1,), (1,)), ((), ())),
                            preferred_element_type=jnp.float32,
                        )
                        scores = jnp.where(seen, scores, -1e30)
                        top = jnp.max(scores, axis=-1, keepdims=True)
                        weights = jnp.exp(scores - top)
                        weights = weights * (1.0 / jnp.sum(weights, axis=-1, keepdims=True))
                        term = jnp.dot(
                            weights.astype(jnp.bfloat16),
                            v_pad[kv * 2 + which, :keys, :],
                            preferred_element_type=jnp.float32,
                        )
                        total = term if total is None else total + term
                    heads[b, :, pl.ds(pl.multiple_of(p * half, half), half)] = total.astype(
                        jnp.bfloat16
                    )
                    return carry

                lax.fori_loop(0, pairs, pair, 0)

    def part(block, c):
        acc = jnp.dot(heads[block], w_out[c], preferred_element_type=jnp.float32)
        return acc.astype(jnp.bfloat16)

    def far_copy(c, way):
        return pltpu.make_async_remote_copy(
            src_ref=far_send.at[c],
            dst_ref=relay_in.at[c],
            send_sem=far_s.at[c],
            recv_sem=far_r.at[c],
            device_id={"tensor": to[way]},
            device_id_type=MESH,
        )

    def near_copy(way, c):
        return pltpu.make_async_remote_copy(
            src_ref=near_send.at[way, c],
            dst_ref=final_in.at[way, c],
            send_sem=near_s.at[way, c],
            recv_sem=near_r.at[way, c],
            device_id={"tensor": to[way]},
            device_id_type=MESH,
        )

    def out_copy(c):
        return pltpu.make_async_remote_copy(
            src_ref=mixed.at[c],
            dst_ref=block_in.at[c],
            send_sem=out_s.at[c],
            recv_sem=out_r.at[c],
            device_id={"section": nxt},
            device_id_type=MESH,
        )

    for copy in loads:
        copy.wait()
    project(me)

    def arrived(way, p):
        place = rows_all.at[source[way], pl.ds(p * piece, piece)]
        return pltpu.make_async_remote_copy(
            src_ref=place,
            dst_ref=place,
            send_sem=ag_s.at[way, p],
            recv_sem=ag_r.at[way, p],
            device_id={"tensor": to[way]},
            device_id_type=MESH,
        )

    def far_arrived(p):
        place = rows_all.at[far, pl.ds(p * piece, piece)]
        return pltpu.make_async_remote_copy(
            src_ref=place,
            dst_ref=place,
            send_sem=fw_s.at[p],
            recv_sem=fw_r.at[p],
            device_id={"tensor": right},
            device_id_type=MESH,
        )

    for p in range(PIECES // 2):
        q = PIECES - 1 - p
        arrived(0, p).wait_recv()
        pass_copy(p).start()
        arrived(1, q).wait_recv()
        pass_copy(q).start()
    for copy in out_loads:
        copy.wait()
    load_mix.wait()
    for p in range(PIECES // 2):
        arrived(0, PIECES - 1 - p).wait_recv()
        arrived(1, p).wait_recv()
    for near in (left, right):
        project(near)
    attend(me, far > me)

    for p in range(PIECES):
        far_arrived(p).wait_recv()
    project(far)
    attend(far, True)

    def far_step(i, carry):
        far_send[i] = part(far, i)
        far_copy(i, 1).start()
        far_send[side + i] = part(far, side + i)
        far_copy(side + i, 0).start()
        return carry

    lax.fori_loop(0, side, far_step, 0)

    attend(right, True)
    attend(left, True)

    def near_step(i, carry):
        for way in range(2):
            relay = side + i if way == 0 else i
            direct = i if way == 0 else side + i
            value = part(to[way], relay)
            far_copy(relay, way).wait_recv()
            total = value.astype(jnp.float32) + relay_in[relay].astype(jnp.float32)
            near_send[way, relay] = total.astype(jnp.bfloat16)
            near_copy(way, relay).start()
            near_send[way, direct] = part(to[way], direct)
            near_copy(way, direct).start()
        return carry

    lax.fori_loop(0, side, near_step, 0)
    attend(me, far < me)

    def own_step(c, carry):
        own_part[c] = part(me, c)
        return carry

    lax.fori_loop(0, col_chunks, own_step, 0)

    def column(i):
        return (i % 2) * side + i // 2

    def final_step(i, carry):
        c = column(i)
        where = pl.ds(pl.multiple_of(c * cols, cols), cols)
        total = own_part[c].astype(jnp.float32)
        for way in range(2):
            near_copy(way, c).wait_recv()
            total = total + final_in[way, c].astype(jnp.float32)
        block = (x_own[:, where].astype(jnp.float32) + total).astype(jnp.bfloat16)
        mixed[c] = block
        out_copy(c).start()
        return carry

    lax.fori_loop(0, col_chunks, final_step, 0)

    for k in range(1, slots + 1):

        @pl.when(prv >= DILATION_STRIDE * k)
        def _():
            hist_copy(k).wait_recv()

    def store_copy(c):
        return pltpu.make_async_copy(
            block_in.at[c],
            out_hbm.at[0, :, pl.ds(pl.multiple_of(c * cols, cols), cols)],
            store_sem.at[c],
        )

    def mix_step(i, carry):
        c = column(i)
        out_copy(c).wait_recv()
        where = pl.ds(pl.multiple_of(c * cols, cols), cols)
        factors = mix_v[pl.ds(prv, 1), :]
        value = factors[:, 0:1] * block_in[c].astype(jnp.float32)
        for k in range(1, slots + 1):
            past = hist_in[k - 1, :, where].astype(jnp.float32)
            value = value + factors[:, k : k + 1] * past
        block_in[c] = value.astype(jnp.bfloat16)
        store_copy(c).start()
        return carry

    lax.fori_loop(0, col_chunks, mix_step, 0)

    for p in range(PIECES):
        own_copy(0, p).wait_send()
        own_copy(1, p).wait_send()
        pass_copy(p).wait_send()
    for k in range(1, slots + 1):

        @pl.when(section + DILATION_STRIDE * k < sections)
        def _():
            hist_copy(k).wait_send()

    def drain(c, carry):
        far_copy(c, 0).wait_send()
        near_copy(0, c).wait_send()
        near_copy(1, c).wait_send()
        out_copy(c).wait_send()
        store_copy(c).wait()
        return carry

    lax.fori_loop(0, col_chunks, drain, 0)


def solution(mesh):
    sections, tensor = mesh.shape["section"], mesh.shape["tensor"]
    assert tensor == 4
    col_chunks = 8

    def on_device(x, history, wq, wk, wv, wo, mix_weights):
        rows, width = x.shape[1:]
        slots = history.shape[1]
        q_width, kv_width = wq.shape[2], wk.shape[2]
        seq = rows * tensor
        tile = 2 * kv_width
        q_tiles = q_width // tile
        cols = width // col_chunks
        bf16 = jnp.bfloat16
        dma = pltpu.SemaphoreType.DMA
        hbm = pl.BlockSpec(memory_space=pl.ANY)
        return pl.pallas_call(
            functools.partial(tick_kernel, sections),
            out_shape=jax.ShapeDtypeStruct(x.shape, bf16),
            in_specs=[hbm] * 7,
            out_specs=hbm,
            scratch_shapes=[
                pltpu.VMEM((rows, width), bf16),
                pltpu.VMEM((tensor, rows, width), bf16),
                pltpu.VMEM((q_tiles + 1, width, tile), bf16),
                pltpu.VMEM((col_chunks, q_width, cols), bf16),
                pltpu.VMEM((2 * q_tiles, seq, kv_width), bf16),
                pltpu.VMEM((4, seq, kv_width), bf16),
                pltpu.VMEM((4, seq, kv_width), bf16),
                pltpu.VMEM((tensor, rows, q_width), bf16),
                pltpu.VMEM((col_chunks, rows, cols), bf16),
                pltpu.VMEM((col_chunks, rows, cols), bf16),
                pltpu.VMEM((2, col_chunks, rows, cols), bf16),
                pltpu.VMEM((2, col_chunks, rows, cols), bf16),
                pltpu.VMEM((col_chunks, rows, cols), bf16),
                pltpu.VMEM((col_chunks, rows, cols), bf16),
                pltpu.VMEM((col_chunks, rows, cols), bf16),
                pltpu.VMEM((slots, rows, width), bf16),
                pltpu.VMEM(mix_weights.shape, mix_weights.dtype),
                dma((q_tiles + 2,)),
                dma((col_chunks,)),
                dma,
                dma,
                dma((slots,)),
                dma((slots,)),
                dma((2, PIECES)),
                dma((2, PIECES)),
                dma((PIECES,)),
                dma((PIECES,)),
                dma((col_chunks,)),
                dma((col_chunks,)),
                dma((2, col_chunks)),
                dma((2, col_chunks)),
                dma((col_chunks,)),
                dma((col_chunks,)),
                dma((col_chunks,)),
            ],
            compiler_params=pltpu.CompilerParams(
                collective_id=0, has_side_effects=True, vmem_limit_bytes=60 * 1024 * 1024
            ),
        )(x, history, wq, wk, wv, wo, mix_weights)

    placed = (
        P("section", "tensor", None),
        P("section", None, "tensor", None),
        P("section", None, "tensor"),
        P("section", None, "tensor"),
        P("section", None, "tensor"),
        P("section", "tensor", None),
        P(),
    )
    return jax.shard_map(
        on_device,
        mesh=mesh,
        in_specs=placed,
        out_specs=P("section", "tensor", None),
        check_vma=False,
    )
```

time: 173 us -> 128 us (0.74)
  the two profiles are of different devices: /device:TPU:10 before, /device:TPU:89 now
where the time goes in v1:
time: 128 us
  Pallas kernels  125 us (98%)
  local copies, waits for them, and re-layouts  3.65 us (3%)
    pallas_call x1, Pallas kernels, on_device(): pl.pallas_call(functools.partial(tick_kernel, sections), out_shape=jax.Sh...  125 us
    unnamed x2, local copies, waits for them, and re-layouts  3.65 us

profile of v1, /device:TPU:89, one launch (start us, length us, event | category | flops | bytes accessed | tf_op | source)
XLA Modules:
  0.0 128.2 jit_solution(2287479261518660306)
XLA Ops:
  0.0 1.4 %copy.8.mix_hbm = f32[32,8]{1,0:T(8,128)} copy(f32[32,8]{0,1:T(8,128)} %param.13) | data formatting | bytes 2048 | tf_op args[6]
  1.4 124.6 %shard_map.73 = bf16[1,128,4096]{2,1,0:T(8,128)(2,1)} custom-call(bf16[1,128,4096]{2,1,0:T(8,128)(2,1)} %x_hbm.1, bf16[1,7,128,4096]{3,2,1,0:T(8,128)(2,1)} %hist_hbm.1, bf16[1,4096,768]{2,1,0:T(8,128)(2,1)} %wq_hbm.1, bf16[1,4096,128]{2,1,0:T(8,128)(2,1)} %wk_hbm.1, bf16[1,4096,128]{2,1,0:T(8,128)(2,1)} %wv_hbm.1, bf16[1,768,4096]{2,1,0:T(8,128)(2,1)} %wo_hbm.1, ...), custom_call_target="tpu_custom_call" | custom-call | tf_op jit(solution)/shard_map/pallas_call | solution.py:467
  126.0 2.3 %copy.10 = bf16[1,128,4096]{2,1,0:T(8,128)(2,1)} copy(bf16[1,128,4096]{2,1,0:T(8,128)(2,1)} %shard_map.73) | data formatting | bytes 2097152

commit v2 on v1

--- a/solution.py
+++ b/solution.py
@@ -9,7 +9,7 @@
 from jax.sharding import PartitionSpec as P
 
 HEAD_DIM = 64
-DILATION_STRIDE = 4
+WIDE_CHUNKS = 5
 MESH = pl.DeviceIdType.MESH
 PIECES = 4
 
@@ -43,15 +43,31 @@
     final_in,
     own_part,
     mixed,
-    block_in,
-    hist_in,
+    even,
+    cross_in,
+    part_out,
+    part_in,
+    raw_a,
+    raw_b,
+    first,
+    pair_out,
+    pair_in,
+    past,
     mix_v,
     w_sem,
     wo_sem,
     x_sem,
     mix_sem,
-    hist_s,
-    hist_r,
+    even_sem,
+    first_sem,
+    cross_s,
+    cross_r,
+    part_s,
+    part_r,
+    raw_s,
+    raw_r,
+    pair_s,
+    pair_r,
     ag_s,
     ag_r,
     fw_s,
@@ -62,7 +78,6 @@
     near_r,
     out_s,
     out_r,
-    store_sem,
 ):
     section = lax.axis_index("section")
     me = lax.axis_index("tensor")
@@ -70,7 +85,6 @@
     to = (right, left)
     source = (left, right)
     rows, width = x_own.shape
-    slots = hist_in.shape[0]
     piece = rows // PIECES
     q_tiles = w_all.shape[0] - 1
     tile = w_all.shape[2]
@@ -84,29 +98,11 @@
     barrier = pltpu.get_barrier_semaphore()
     for other in to:
         pl.semaphore_signal(barrier, inc=1, device_id={"tensor": other}, device_id_type=MESH)
-    for other in (nxt, prv):
+    row, col = section // 8, lax.rem(section // 4, 2)
+    partner = section + 4 - 8 * col
+    others = [lax.rem(section + 8 * d, sections) for d in (1, 2, 3)]
+    for other in (nxt, prv, partner, *others):
         pl.semaphore_signal(barrier, inc=1, device_id={"section": other}, device_id_type=MESH)
-    expected = jnp.int32(4)
-    for k in range(1, slots + 1):
-        step = DILATION_STRIDE * k
-        forward, backward = section + step < sections, prv >= step
-
-        @pl.when(forward)
-        def _():
-            pl.semaphore_signal(
-                barrier,
-                inc=1,
-                device_id={"section": lax.rem(section + step + 1, sections)},
-                device_id_type=MESH,
-            )
-
-        @pl.when(backward)
-        def _():
-            pl.semaphore_signal(
-                barrier, inc=1, device_id={"section": prv - step}, device_id_type=MESH
-            )
-
-        expected = expected + forward.astype(jnp.int32) + backward.astype(jnp.int32)
 
     loads = []
     for j in range(q_tiles):
@@ -138,7 +134,7 @@
         return carry
 
     lax.fori_loop(0, rows // 16, norm_rows, 0)
-    pl.semaphore_wait(barrier, expected)
+    pl.semaphore_wait(barrier, 8)
 
     def own_copy(way, p):
         place = rows_all.at[me, pl.ds(p * piece, piece)]
@@ -167,26 +163,83 @@
         own_copy(0, p).start()
         own_copy(1, PIECES - 1 - p).start()
 
-    def hist_copy(k):
+    wide = even.shape[2]
+    wide_chunks = wide // cols
+    narrow_chunks = col_chunks - wide_chunks
+    lead, tail = pl.ds(0, wide), pl.ds(wide, width - wide)
+    steps = range(1, 4)
+
+    def onward(d):
+        return row + d < 4
+
+    def inward(d):
+        return row >= d
+
+    def cross_sent(d):
+        return onward(d) if d else col == 0
+
+    def cross_due(d):
+        return onward(d) if d else col == 1
+
+    def section_copy(src, dst, send, recv, target):
         return pltpu.make_async_remote_copy(
-            src_ref=hist_hbm.at[0, k - 1],
-            dst_ref=hist_in.at[k - 1],
-            send_sem=hist_s.at[k - 1],
-            recv_sem=hist_r.at[k - 1],
-            device_id={"section": lax.rem(section + DILATION_STRIDE * k + 1, sections)},
+            src_ref=src,
+            dst_ref=dst,
+            send_sem=send,
+            recv_sem=recv,
+            device_id={"section": target},
             device_id_type=MESH,
         )
 
-    for k in range(1, slots + 1):
-        step = DILATION_STRIDE * k
-
-        @pl.when(section + step < sections)
-        def _():
-            hist_copy(k).start()
-
-        @pl.when(prv < step)
-        def _():
-            hist_in[k - 1] = jnp.zeros((rows, width), hist_in.dtype)
+    def cross_copy(d):
+        return section_copy(
+            hist_hbm.at[0, jnp.maximum(2 * d - 2 * col, 0), :, lead],
+            cross_in.at[d],
+            cross_s.at[d],
+            cross_r.at[d],
+            partner,
+        )
+
+    def part_copy(d):
+        return section_copy(
+            part_out.at[d - 1], part_in.at[d - 1], part_s.at[d - 1], part_r.at[d - 1], others[d - 1]
+        )
+
+    def raw_copy(d, which):
+        slot = 2 * d - 1 if which == 0 else 2 * d - 2 * col
+        return section_copy(
+            hist_hbm.at[0, slot, :, tail],
+            (raw_a, raw_b)[which].at[d - 1],
+            raw_s.at[which, d - 1],
+            raw_r.at[which, d - 1],
+            others[d - 1],
+        )
+
+    def pair_copy():
+        return section_copy(pair_out, pair_in, pair_s, pair_r, partner)
+
+    pair_sent = (row >= 1) | (col == 0)
+    pair_due = (row >= 1) | (col == 1)
+
+    def even_load(d):
+        return pltpu.make_async_copy(
+            hist_hbm.at[0, 2 * d - 1, :, lead], even.at[d - 1], even_sem.at[d - 1]
+        )
+
+    first_load = pltpu.make_async_copy(hist_hbm.at[0, 0, :, tail], first, first_sem)
+
+    for d in (1, 2, 3, 0):
+
+        @pl.when(cross_sent(d))
+        def _():
+            cross_copy(d).start()
+
+    for d in steps:
+
+        @pl.when(onward(d))
+        def _():
+            raw_copy(d, 1).start()
+            raw_copy(d, 0).start()
 
     out_loads = []
     for c in range(col_chunks):
@@ -197,6 +250,126 @@
                 )
             )
         )
+
+    for d in steps:
+
+        @pl.when(onward(d))
+        def _():
+            even_load(d).start()
+
+        @pl.when(row < d)
+        def _():
+            part_in[d - 1] = jnp.zeros(part_in.shape[1:], part_in.dtype)
+            raw_a[d - 1] = jnp.zeros(raw_a.shape[1:], raw_a.dtype)
+            raw_b[d - 1] = jnp.zeros(raw_b.shape[1:], raw_b.dtype)
+
+    @pl.when(col == 0)
+    def _():
+        first_load.start()
+        cross_in[0] = jnp.zeros(cross_in.shape[1:], cross_in.dtype)
+
+    @pl.when(col == 1)
+    def _():
+        first[...] = jnp.zeros(first.shape, first.dtype)
+
+    @pl.when(jnp.logical_not(pair_due))
+    def _():
+        pair_in[...] = jnp.zeros(pair_in.shape, pair_in.dtype)
+
+    def weight(target, k):
+        table = mix_v[...]
+        at = (lax.broadcasted_iota(jnp.int32, table.shape, 0) == k) & (
+            lax.broadcasted_iota(jnp.int32, table.shape, 1) == target
+        )
+        return jnp.sum(jnp.where(at, table, 0.0), keepdims=True)
+
+    def chunk(c):
+        return pl.ds(pl.multiple_of(c * cols, cols), cols)
+
+    def relay(d):
+        @pl.when(onward(d))
+        def _():
+            with jax.named_scope(f"relay{d}"):
+                own_weight = weight(section + 8 * d, 2 * d)
+                partner_weight = weight(section + 8 * d, 2 * d - 1 + 2 * col)
+                even_load(d).wait()
+                cross_copy(d).wait_recv()
+
+                def add(c, carry):
+                    at = chunk(c)
+                    value = own_weight * even[d - 1, :, at].astype(jnp.float32)
+                    value = value + partner_weight * cross_in[d, :, at].astype(jnp.float32)
+                    part_out[d - 1, :, at] = value.astype(jnp.bfloat16)
+                    return carry
+
+                lax.fori_loop(0, wide_chunks, add, 0)
+                part_copy(d).start()
+
+    def relay_pair():
+        @pl.when(col == 0)
+        def _():
+            first_load.wait()
+
+        for d in steps:
+
+            @pl.when(inward(d))
+            def _():
+                raw_copy(d, 1).wait_recv()
+
+        @pl.when(pair_sent)
+        def _():
+            weights = [weight(partner, 2 * d + 1 - 2 * col) for d in steps]
+            first_weight = weight(partner, 1)
+
+            def add(c, carry):
+                at = chunk(c)
+                value = first_weight * first[:, at].astype(jnp.float32)
+                for d in steps:
+                    value = value + weights[d - 1] * raw_b[d - 1, :, at].astype(jnp.float32)
+                pair_out[:, at] = value.astype(jnp.bfloat16)
+                return carry
+
+            lax.fori_loop(0, narrow_chunks, add, 0)
+            pair_copy().start()
+
+    def gather_past():
+        @pl.when(col == 1)
+        def _():
+            cross_copy(0).wait_recv()
+
+        for d in steps:
+
+            @pl.when(inward(d))
+            def _():
+                part_copy(d).wait_recv()
+                raw_copy(d, 0).wait_recv()
+
+        @pl.when(pair_due)
+        def _():
+            pair_copy().wait_recv()
+
+        cross_weight = weight(section, 1)
+
+        def add_wide(c, carry):
+            at = chunk(c)
+            value = cross_weight * cross_in[0, :, at].astype(jnp.float32)
+            for d in steps:
+                value = value + part_in[d - 1, :, at].astype(jnp.float32)
+            past[c] = value
+            return carry
+
+        lax.fori_loop(0, wide_chunks, add_wide, 0)
+        weights = [weight(section, 2 * d) for d in steps]
+
+        def add_narrow(c, carry):
+            at = chunk(c)
+            value = pair_in[:, at].astype(jnp.float32)
+            for d in steps:
+                value = value + weights[d - 1] * raw_a[d - 1, :, at].astype(jnp.float32)
+            past[wide_chunks + c] = value
+            return carry
+
+        lax.fori_loop(0, narrow_chunks, add_narrow, 0)
 
     scale = 1.0 / math.sqrt(HEAD_DIM)
 
@@ -294,7 +467,7 @@
     def out_copy(c):
         return pltpu.make_async_remote_copy(
             src_ref=mixed.at[c],
-            dst_ref=block_in.at[c],
+            dst_ref=out_hbm.at[0, :, pl.ds(pl.multiple_of(c * cols, cols), cols)],
             send_sem=out_s.at[c],
             recv_sem=out_r.at[c],
             device_id={"section": nxt},
@@ -336,12 +509,15 @@
     for copy in out_loads:
         copy.wait()
     load_mix.wait()
+    with jax.named_scope("relays"):
+        relay(1)
     for p in range(PIECES // 2):
         arrived(0, PIECES - 1 - p).wait_recv()
         arrived(1, p).wait_recv()
     for near in (left, right):
         project(near)
     attend(me, far > me)
+    relay(2)
 
     for p in range(PIECES):
         far_arrived(p).wait_recv()
@@ -356,6 +532,9 @@
         return carry
 
     lax.fori_loop(0, side, far_step, 0)
+    relay(3)
+    with jax.named_scope("relay_pair"):
+        relay_pair()
 
     attend(right, True)
     attend(left, True)
@@ -382,6 +561,10 @@
 
     lax.fori_loop(0, col_chunks, own_step, 0)
 
+    with jax.named_scope("past"):
+        gather_past()
+    own_weight = weight(section, 0)
+
     def column(i):
         return (i % 2) * side + i // 2
 
@@ -393,56 +576,39 @@
             near_copy(way, c).wait_recv()
             total = total + final_in[way, c].astype(jnp.float32)
         block = (x_own[:, where].astype(jnp.float32) + total).astype(jnp.bfloat16)
-        mixed[c] = block
+        mixed[c] = (own_weight * block.astype(jnp.float32) + past[c]).astype(jnp.bfloat16)
         out_copy(c).start()
         return carry
 
     lax.fori_loop(0, col_chunks, final_step, 0)
-
-    for k in range(1, slots + 1):
-
-        @pl.when(prv >= DILATION_STRIDE * k)
-        def _():
-            hist_copy(k).wait_recv()
-
-    def store_copy(c):
-        return pltpu.make_async_copy(
-            block_in.at[c],
-            out_hbm.at[0, :, pl.ds(pl.multiple_of(c * cols, cols), cols)],
-            store_sem.at[c],
-        )
-
-    def mix_step(i, carry):
-        c = column(i)
-        out_copy(c).wait_recv()
-        where = pl.ds(pl.multiple_of(c * cols, cols), cols)
-        factors = mix_v[pl.ds(prv, 1), :]
-        value = factors[:, 0:1] * block_in[c].astype(jnp.float32)
-        for k in range(1, slots + 1):
-            past = hist_in[k - 1, :, where].astype(jnp.float32)
-            value = value + factors[:, k : k + 1] * past
-        block_in[c] = value.astype(jnp.bfloat16)
-        store_copy(c).start()
-        return carry
-
-    lax.fori_loop(0, col_chunks, mix_step, 0)
 
     for p in range(PIECES):
         own_copy(0, p).wait_send()
         own_copy(1, p).wait_send()
         pass_copy(p).wait_send()
-    for k in range(1, slots + 1):
-
-        @pl.when(section + DILATION_STRIDE * k < sections)
-        def _():
-            hist_copy(k).wait_send()
+    for d in (0, *steps):
+
+        @pl.when(cross_sent(d))
+        def _():
+            cross_copy(d).wait_send()
+
+    for d in steps:
+
+        @pl.when(onward(d))
+        def _():
+            part_copy(d).wait_send()
+            raw_copy(d, 0).wait_send()
+            raw_copy(d, 1).wait_send()
+
+    @pl.when(pair_sent)
+    def _():
+        pair_copy().wait_send()
 
     def drain(c, carry):
         far_copy(c, 0).wait_send()
         near_copy(0, c).wait_send()
         near_copy(1, c).wait_send()
-        out_copy(c).wait_send()
-        store_copy(c).wait()
+        out_copy(c).wait()
         return carry
 
     lax.fori_loop(0, col_chunks, drain, 0)
@@ -450,17 +616,17 @@
 
 def solution(mesh):
     sections, tensor = mesh.shape["section"], mesh.shape["tensor"]
-    assert tensor == 4
+    assert tensor == 4 and sections == 32
     col_chunks = 8
 
     def on_device(x, history, wq, wk, wv, wo, mix_weights):
         rows, width = x.shape[1:]
-        slots = history.shape[1]
         q_width, kv_width = wq.shape[2], wk.shape[2]
         seq = rows * tensor
         tile = 2 * kv_width
         q_tiles = q_width // tile
         cols = width // col_chunks
+        wide = WIDE_CHUNKS * cols
         bf16 = jnp.bfloat16
         dma = pltpu.SemaphoreType.DMA
         hbm = pl.BlockSpec(memory_space=pl.ANY)
@@ -484,15 +650,31 @@
                 pltpu.VMEM((2, col_chunks, rows, cols), bf16),
                 pltpu.VMEM((col_chunks, rows, cols), bf16),
                 pltpu.VMEM((col_chunks, rows, cols), bf16),
-                pltpu.VMEM((col_chunks, rows, cols), bf16),
-                pltpu.VMEM((slots, rows, width), bf16),
-                pltpu.VMEM(mix_weights.shape, mix_weights.dtype),
+                pltpu.VMEM((3, rows, wide), bf16),
+                pltpu.VMEM((4, rows, wide), bf16),
+                pltpu.VMEM((3, rows, wide), bf16),
+                pltpu.VMEM((3, rows, wide), bf16),
+                pltpu.VMEM((3, rows, width - wide), bf16),
+                pltpu.VMEM((3, rows, width - wide), bf16),
+                pltpu.VMEM((rows, width - wide), bf16),
+                pltpu.VMEM((rows, width - wide), bf16),
+                pltpu.VMEM((rows, width - wide), bf16),
+                pltpu.VMEM((col_chunks, rows, cols), jnp.float32),
+                pltpu.VMEM(mix_weights.shape[::-1], mix_weights.dtype),
                 dma((q_tiles + 2,)),
                 dma((col_chunks,)),
                 dma,
                 dma,
-                dma((slots,)),
-                dma((slots,)),
+                dma((3,)),
+                dma,
+                dma((4,)),
+                dma((4,)),
+                dma((3,)),
+                dma((3,)),
+                dma((2, 3)),
+                dma((2, 3)),
+                dma,
+                dma,
                 dma((2, PIECES)),
                 dma((2, PIECES)),
                 dma((PIECES,)),
@@ -503,12 +685,11 @@
                 dma((2, col_chunks)),
                 dma((col_chunks,)),
                 dma((col_chunks,)),
-                dma((col_chunks,)),
             ],
             compiler_params=pltpu.CompilerParams(
                 collective_id=0, has_side_effects=True, vmem_limit_bytes=60 * 1024 * 1024
             ),
-        )(x, history, wq, wk, wv, wo, mix_weights)
+        )(x, history, wq, wk, wv, wo, mix_weights.T)
 
     placed = (
         P("section", "tensor", None),

time: 128 us -> 92.7 us (0.72)
  the two profiles are of different devices: /device:TPU:89 before, /device:TPU:2 now
where the time goes in v2:
time: 92.7 us; the launch traced here: 92.5 us
  Pallas kernels  90.2 us (97%)
  local copies, waits for them, and re-layouts  2.29 us (2%)
    pallas_call x1, Pallas kernels, on_device(): pl.pallas_call(functools.partial(tick_kernel, sections), out_shape=jax.Sh...  90.2 us
    unnamed x1, local copies, waits for them, and re-layouts  2.29 us

profile of v2, /device:TPU:2, one launch (start us, length us, event | category | flops | bytes accessed | tf_op | source)
XLA Modules:
  0.0 92.5 jit_solution(10966802680072508899)
XLA Ops:
  0.0 90.2 %shard_map.73 = bf16[1,128,4096]{2,1,0:T(8,128)(2,1)} custom-call(bf16[1,128,4096]{2,1,0:T(8,128)(2,1)} %x_hbm.1, bf16[1,7,128,4096]{3,2,1,0:T(8,128)(2,1)} %hist_hbm.1, bf16[1,4096,768]{2,1,0:T(8,128)(2,1)} %wq_hbm.1, bf16[1,4096,128]{2,1,0:T(8,128)(2,1)} %wk_hbm.1, bf16[1,4096,128]{2,1,0:T(8,128)(2,1)} %wv_hbm.1, bf16[1,768,4096]{2,1,0:T(8,128)(2,1)} %wo_hbm.1, ...), custom_call_target="tpu_custom_call" | custom-call | tf_op jit(solution)/shard_map/pallas_call | solution.py:633
  90.2 2.3 %copy.9 = bf16[1,128,4096]{2,1,0:T(8,128)(2,1)} copy(bf16[1,128,4096]{2,1,0:T(8,128)(2,1)} %shard_map.73) | data formatting | bytes 2097152

commit v3 on v2

v3 whole, which is shorter than its diff:
```python
import functools
import math

import jax
import jax.numpy as jnp
from jax import lax
from jax.experimental import pallas as pl
from jax.experimental.pallas import tpu as pltpu
from jax.sharding import PartitionSpec as P

HEAD_DIM = 64
SUMMED = (4, 0, 5, 1, 3)
PLAIN = (6, 2, 7)
MESH = pl.DeviceIdType.MESH
PIECES = 4


def start(copy):
    copy.start()
    return copy


def tick_kernel(
    sections,
    x_hbm,
    hist_hbm,
    wq_hbm,
    wk_hbm,
    wv_hbm,
    wo_hbm,
    mix_hbm,
    out_hbm,
    x_own,
    rows_all,
    w_all,
    w_out,
    q_all,
    k_pad,
    v_pad,
    heads,
    far_send,
    relay_in,
    near_send,
    final_in,
    own_part,
    mixed,
    even,
    cross_in,
    part_out,
    part_in,
    raw_a,
    raw_b,
    first,
    pair_out,
    pair_in,
    past,
    mix_v,
    w_sem,
    wo_sem,
    x_sem,
    mix_sem,
    even_sem,
    first_sem,
    cross_s,
    cross_r,
    part_s,
    part_r,
    raw_s,
    raw_r,
    pair_s,
    pair_r,
    ag_s,
    ag_r,
    fw_s,
    fw_r,
    far_s,
    far_r,
    near_s,
    near_r,
    out_s,
    out_r,
):
    section = lax.axis_index("section")
    me = lax.axis_index("tensor")
    right, left, far = lax.rem(me + 1, 4), lax.rem(me + 3, 4), lax.rem(me + 2, 4)
    to = (right, left)
    source = (left, right)
    rows, width = x_own.shape
    piece = rows // PIECES
    q_tiles = w_all.shape[0] - 1
    tile = w_all.shape[2]
    half = tile // 2
    col_chunks, _, cols = w_out.shape
    side = col_chunks // 2
    nxt = lax.rem(section + 1, sections)
    prv = lax.rem(section + sections - 1, sections)

    def load_x(p):
        at = pl.ds(p * piece, piece)
        return pltpu.make_async_copy(x_hbm.at[0, at], x_own.at[at], x_sem.at[p])

    for p in range(PIECES):
        load_x(p).start()
    barrier = pltpu.get_barrier_semaphore()
    for other in to:
        pl.semaphore_signal(barrier, inc=1, device_id={"tensor": other}, device_id_type=MESH)
    row, col = section // 8, lax.rem(section // 4, 2)
    partner = section + 4 - 8 * col
    others = [lax.rem(section + 8 * d, sections) for d in (1, 2, 3)]
    for other in (nxt, prv, partner, *others):
        pl.semaphore_signal(barrier, inc=1, device_id={"section": other}, device_id_type=MESH)

    loads = []
    for j in range(q_tiles):
        loads.append(
            pltpu.make_async_copy(
                wq_hbm.at[0, :, pl.ds(j * tile, tile)], w_all.at[j], w_sem.at[j]
            )
        )
    loads.append(
        pltpu.make_async_copy(
            wk_hbm.at[0], w_all.at[q_tiles, :, pl.ds(0, half)], w_sem.at[q_tiles]
        )
    )
    loads.append(
        pltpu.make_async_copy(
            wv_hbm.at[0], w_all.at[q_tiles, :, pl.ds(half, half)], w_sem.at[q_tiles + 1]
        )
    )
    load_x(0).wait()
    for copy in loads:
        copy.start()
    load_mix = start(pltpu.make_async_copy(mix_hbm, mix_v, mix_sem))

    def own_copy(way, p):
        place = rows_all.at[me, pl.ds(p * piece, piece)]
        return pltpu.make_async_remote_copy(
            src_ref=place,
            dst_ref=place,
            send_sem=ag_s.at[way],
            recv_sem=ag_r.at[way, p],
            device_id={"tensor": to[way]},
            device_id_type=MESH,
        )

    def settle(ref, send, recv):
        return pltpu.make_async_remote_copy(
            src_ref=ref,
            dst_ref=ref,
            send_sem=send,
            recv_sem=recv,
            device_id={"tensor": right},
            device_id_type=MESH,
        )

    def passed(way, p, block):
        place = rows_all.at[
            block, pl.ds(p * piece, piece), pl.ds(way * (width // 2), width // 2)
        ]
        return pltpu.make_async_remote_copy(
            src_ref=place,
            dst_ref=place,
            send_sem=fw_s.at[way],
            recv_sem=fw_r.at[way, p],
            device_id={"tensor": to[way]},
            device_id_type=MESH,
        )

    def pass_copy(way, p):
        return passed(way, p, source[way])

    def norm_piece(p):
        def norm_rows(i, carry):
            at = pl.ds(pl.multiple_of(p * piece + i * 16, 16), 16)
            values = x_own[at, :].astype(jnp.float32)
            inv = lax.rsqrt(jnp.mean(values * values, axis=-1, keepdims=True) + 1e-05)
            rows_all[me, at, :] = (values * inv).astype(jnp.bfloat16)
            return carry

        lax.fori_loop(0, piece // 16, norm_rows, 0)

    norm_piece(0)
    pl.semaphore_wait(barrier, 8)
    for p in range(PIECES):
        if p:
            load_x(p).wait()
            norm_piece(p)
        own_copy(0, p).start()
        own_copy(1, p).start()

    steps = range(1, 4)

    def chunk(c):
        return pl.ds(c * cols, cols)

    def onward(d):
        return row + d < 4

    def inward(d):
        return row >= d

    def cross_sent(d):
        return onward(d) if d else col == 0

    def cross_due(d):
        return onward(d) if d else col == 1

    def section_copy(src, dst, send, recv, target):
        return pltpu.make_async_remote_copy(
            src_ref=src,
            dst_ref=dst,
            send_sem=send,
            recv_sem=recv,
            device_id={"section": target},
            device_id_type=MESH,
        )

    def cross_copy(d, j):
        return section_copy(
            hist_hbm.at[0, jnp.maximum(2 * d - 2 * col, 0), :, chunk(SUMMED[j])],
            cross_in.at[d, j],
            cross_s.at[d],
            cross_r.at[d, j],
            partner,
        )

    def part_copy(d, j):
        return section_copy(
            part_out.at[d - 1, j],
            part_in.at[d - 1, j],
            part_s.at[d - 1],
            part_r.at[d - 1, j],
            others[d - 1],
        )

    def raw_copy(d, which, n):
        slot = 2 * d - 1 if which == 0 else 2 * d - 2 * col
        return section_copy(
            hist_hbm.at[0, slot, :, chunk(PLAIN[n])],
            (raw_a, raw_b)[which].at[d - 1, n],
            raw_s.at[which, d - 1],
            raw_r.at[which, d - 1],
            others[d - 1],
        )

    def pair_copy(n):
        return section_copy(pair_out.at[n], pair_in.at[n], pair_s, pair_r.at[n], partner)

    pair_sent = (row >= 1) | (col == 0)
    pair_due = (row >= 1) | (col == 1)

    def even_load(d):
        return pltpu.make_async_copy(
            hist_hbm.at[0, 2 * d - 1], even.at[d - 1], even_sem.at[d - 1]
        )

    first_load = pltpu.make_async_copy(hist_hbm.at[0, 0], first, first_sem)

    def cross(some):
        for j in some:
            for d in (1, 2, 3, 0):

                @pl.when(cross_sent(d))
                def _():
                    cross_copy(d, j).start()

    cross(range(len(SUMMED)))

    for which in (1, 0):
        for d in steps:

            @pl.when(onward(d))
            def _():
                for n in range(len(PLAIN)):
                    raw_copy(d, which, n).start()

    out_loads = []
    for c in range(col_chunks):
        out_loads.append(
            start(
                pltpu.make_async_copy(
                    wo_hbm.at[0, :, pl.ds(c * cols, cols)], w_out.at[c], wo_sem.at[c]
                )
            )
        )

    for d in steps:

        @pl.when(onward(d))
        def _():
            even_load(d).start()

        @pl.when(row < d)
        def _():
            part_in[d - 1] = jnp.zeros(part_in.shape[1:], part_in.dtype)
            raw_a[d - 1] = jnp.zeros(raw_a.shape[1:], raw_a.dtype)
            raw_b[d - 1] = jnp.zeros(raw_b.shape[1:], raw_b.dtype)

    @pl.when(col == 0)
    def _():
        first_load.start()
        cross_in[0] = jnp.zeros(cross_in.shape[1:], cross_in.dtype)

    @pl.when(col == 1)
    def _():
        first[...] = jnp.zeros(first.shape, first.dtype)

    @pl.when(jnp.logical_not(pair_due))
    def _():
        pair_in[...] = jnp.zeros(pair_in.shape, pair_in.dtype)

    k_pad[...] = jnp.zeros(k_pad.shape, k_pad.dtype)
    for f in range(v_pad.shape[0]):
        v_pad[f, :, :half] = jnp.zeros((v_pad.shape[1], half), v_pad.dtype)
        v_pad[f, :, half:] = jnp.ones((v_pad.shape[1], half), v_pad.dtype)

    def weight(target, k):
        table = mix_v[...]
        at = (lax.broadcasted_iota(jnp.int32, table.shape, 0) == k) & (
            lax.broadcasted_iota(jnp.int32, table.shape, 1) == target
        )
        return jnp.sum(jnp.where(at, table, 0.0), keepdims=True)

    def relay(j):
        for d in steps:

            @pl.when(onward(d))
            def _():
                own_weight = weight(section + 8 * d, 2 * d)
                partner_weight = weight(section + 8 * d, 2 * d - 1 + 2 * col)
                if j == 0:
                    even_load(d).wait()
                cross_copy(d, j).wait_recv()
                value = own_weight * even[d - 1, :, chunk(SUMMED[j])].astype(jnp.float32)
                value = value + partner_weight * cross_in[d, j].astype(jnp.float32)
                part_out[d - 1, j] = value.astype(jnp.bfloat16)
                part_copy(d, j).start()

    def relay_pair():
        @pl.when(col == 0)
        def _():
            first_load.wait()

        for d in steps:

            @pl.when(inward(d))
            def _():
                settle(raw_b.at[d - 1], raw_s.at[1, d - 1], raw_r.at[1, d - 1]).wait_recv()

        @pl.when(pair_sent)
        def _():
            weights = [weight(partner, 2 * d + 1 - 2 * col) for d in steps]
            first_weight = weight(partner, 1)
            for n, c in enumerate(PLAIN):
                value = first_weight * first[:, chunk(c)].astype(jnp.float32)
                for d in steps:
                    value = value + weights[d - 1] * raw_b[d - 1, n].astype(jnp.float32)
                pair_out[n] = value.astype(jnp.bfloat16)
                pair_copy(n).start()

    def gather_past(c):
        if c in SUMMED:
            j = SUMMED.index(c)

            @pl.when(col == 1)
            def _():
                cross_copy(0, j).wait_recv()

            for d in steps:

                @pl.when(inward(d))
                def _():
                    part_copy(d, j).wait_recv()

            value = weight(section, 1) * cross_in[0, j].astype(jnp.float32)
            for d in steps:
                value = value + part_in[d - 1, j].astype(jnp.float32)
        else:
            n = PLAIN.index(c)

            @pl.when(pair_due)
            def _():
                pair_copy(n).wait_recv()

            if n == 0:
                for d in steps:

                    @pl.when(inward(d))
                    def _():
                        settle(raw_a.at[d - 1], raw_s.at[0, d - 1], raw_r.at[0, d - 1]).wait_recv()

            value = pair_in[n].astype(jnp.float32)
            for d in steps:
                value = value + weight(section, 2 * d) * raw_a[d - 1, n].astype(jnp.float32)
        past[c] = value

    scale = 1.0 / math.sqrt(HEAD_DIM)

    def project(spans):
        def places():
            done = 0
            for block, first_row, size in spans:
                where = pl.ds(pl.multiple_of(block * rows + first_row, size), size)
                yield where, slice(done, done + size)
                done += size

        def tokens():
            taken = [rows_all[block, at : at + size, :] for block, at, size in spans]
            return taken[0] if len(taken) == 1 else jnp.concatenate(taken, axis=0)

        def q_tile(j, carry):
            acc = jnp.dot(tokens(), w_all[j], preferred_element_type=jnp.float32)
            acc = acc.astype(jnp.bfloat16) * jnp.bfloat16(scale)
            for where, got in places():
                q_all[2 * j, where, :] = acc[got, :half]
                q_all[2 * j + 1, where, :] = acc[got, half:]
            return carry

        lax.fori_loop(0, q_tiles, q_tile, 0)
        acc = jnp.dot(tokens(), w_all[q_tiles], preferred_element_type=jnp.float32)
        acc = acc.astype(jnp.bfloat16).astype(jnp.float32)
        for values, padded in ((acc[:, :half], k_pad), (acc[:, half:], v_pad)):
            lane = lax.broadcasted_iota(jnp.int32, values.shape, 1)
            turned = pltpu.roll(values, HEAD_DIM, 1)
            low = lane < HEAD_DIM
            zero = jnp.zeros_like(values)
            forms = (
                jnp.where(low, values, zero),
                jnp.where(low, zero, turned),
                jnp.where(low, turned, zero),
                jnp.where(low, zero, values),
            )
            for f, form in enumerate(forms):
                for where, got in places():
                    padded[f, where, pl.ds(0, half)] = form[got].astype(jnp.bfloat16)

    pairs = q_all.shape[0]
    pairs_per_kv = pairs // (half // HEAD_DIM)

    def attend(block, wanted, first_row, size):
        for b in range(4):
            keys = (b + 1) * rows
            at = b * rows + first_row

            @pl.when(wanted & (block == b))
            def _():
                with jax.named_scope(f"att{b}_{size}"):
                    shape = (pairs_per_kv, size, rows)
                    seen = (
                        lax.broadcasted_iota(jnp.int32, shape, 1) + first_row
                        >= lax.broadcasted_iota(jnp.int32, shape, 2)
                    ).reshape(pairs_per_kv * size, rows)
                    for kv in range(pairs // pairs_per_kv):
                        group = slice(kv * pairs_per_kv, (kv + 1) * pairs_per_kv)
                        query = q_all[group, at : at + size, :]
                        query = query.reshape(pairs_per_kv * size, half)
                        total = None
                        for which in range(2):
                            scores = lax.dot_general(
                                query,
                                k_pad[kv * 2 + which, :keys, :],
                                (((1,), (1,)), ((), ())),
                                preferred_element_type=jnp.float32,
                            )
                            last = jnp.where(seen, scores[:, b * rows :], -1e30)
                            if b:
                                scores = jnp.concatenate([scores[:, : b * rows], last], axis=1)
                            else:
                                scores = last
                            top = jnp.max(scores, axis=-1, keepdims=True)
                            weights = jnp.exp(scores - top).astype(jnp.bfloat16)
                            term = jnp.dot(
                                weights,
                                v_pad[kv * 2 + which, :keys, :],
                                preferred_element_type=jnp.float32,
                            )
                            term = term[:, :half] * (1.0 / term[:, half:])
                            total = term if total is None else total + term
                        total = total.astype(jnp.bfloat16)
                        for i in range(pairs_per_kv):
                            p = kv * pairs_per_kv + i
                            heads[b, first_row : first_row + size, p * half : (p + 1) * half] = (
                                total[i * size : (i + 1) * size]
                            )

    def part(block, c, first_row=0, size=rows):
        taken = heads[block, first_row : first_row + size, :]
        acc = jnp.dot(taken, w_out[c], preferred_element_type=jnp.float32)
        return acc.astype(jnp.bfloat16)

    short = rows // 2

    def far_copy(c, h, way):
        at = pl.ds(h * short, short)
        return pltpu.make_async_remote_copy(
            src_ref=far_send.at[c, at],
            dst_ref=relay_in.at[c, at],
            send_sem=far_s,
            recv_sem=far_r.at[c],
            device_id={"tensor": to[way]},
            device_id_type=MESH,
        )

    def near_copy(way, c):
        return pltpu.make_async_remote_copy(
            src_ref=near_send.at[way, c],
            dst_ref=final_in.at[way, c],
            send_sem=near_s,
            recv_sem=near_r.at[way, c],
            device_id={"tensor": to[way]},
            device_id_type=MESH,
        )

    def out_copy(c):
        return pltpu.make_async_remote_copy(
            src_ref=mixed.at[c],
            dst_ref=out_hbm.at[0, :, pl.ds(pl.multiple_of(c * cols, cols), cols)],
            send_sem=out_s,
            recv_sem=out_r,
            device_id={"section": nxt},
            device_id_type=MESH,
        )

    for copy in loads:
        copy.wait()
    project(((me, 0, rows),))

    def arrived(way, p):
        place = rows_all.at[source[way], pl.ds(p * piece, piece)]
        return pltpu.make_async_remote_copy(
            src_ref=place,
            dst_ref=place,
            send_sem=ag_s.at[way],
            recv_sem=ag_r.at[way, p],
            device_id={"tensor": to[way]},
            device_id_type=MESH,
        )

    for p in range(PIECES):
        for way in range(2):
            arrived(way, p).wait_recv()
            pass_copy(way, p).start()
        if p == 1:
            load_mix.wait()
            with jax.named_scope("relay0"):
                relay(0)
    with jax.named_scope("relay1"):
        relay(1)
    for copy in out_loads:
        copy.wait()
    with jax.named_scope("f_proj_near"):
        project(((left, 0, rows), (right, 0, rows)))
    attend(me, far > me, 0, rows)

    for h in range(2):
        for p in (2 * h, 2 * h + 1):
            for way in range(2):
                passed(way, p, far).wait_recv()
        with jax.named_scope(f"i_proj_far{h}"):
            project(((far, h * short, short),))
        with jax.named_scope(f"j_att_far{h}"):
            attend(far, True, h * short, short)

        def far_step(i, carry):
            at = pl.ds(h * short, short)
            far_send[i, at] = part(far, i, h * short, short)
            far_copy(i, h, 1).start()
            far_send[side + i, at] = part(far, side + i, h * short, short)
            far_copy(side + i, h, 0).start()
            return carry

        with jax.named_scope(f"k_far_step{h}"):
            lax.fori_loop(0, side, far_step, 0)
        if h == 0:
            with jax.named_scope("relay2"):
                relay(2)
            with jax.named_scope("relay_pair"):
                relay_pair()

    attend(right, True, 0, rows)
    attend(left, True, 0, rows)
    with jax.named_scope("relay3"):
        relay(3)

    def near_step(i, carry):
        def relayed(way):
            c = side + i if way == 0 else i
            value = part(to[way], c)
            settle(relay_in.at[c], far_s, far_r.at[c]).wait_recv()
            total = value.astype(jnp.float32) + relay_in[c].astype(jnp.float32)
            near_send[way, c] = total.astype(jnp.bfloat16)
            near_copy(way, c).start()

        def direct(way):
            c = i if way == 0 else side + i
            near_send[way, c] = part(to[way], c)
            near_copy(way, c).start()

        relayed(0)
        direct(1)
        relayed(1)
        direct(0)
        return carry

    lax.fori_loop(0, side, near_step, 0)
    attend(me, far < me, 0, rows)

    def own_step(c, carry):
        own_part[c] = part(me, c)
        return carry

    lax.fori_loop(0, col_chunks, own_step, 0)

    own_weight = weight(section, 0)

    for i in range(col_chunks):
        c = (i + 1) % 2 * side + i // 2
        with jax.named_scope(f"past{i}"):
            gather_past(c)
        with jax.named_scope(f"final{i}"):
            total = own_part[c].astype(jnp.float32)
            for way in range(2):
                near_copy(way, c).wait_recv()
                total = total + final_in[way, c].astype(jnp.float32)
            block = (x_own[:, chunk(c)].astype(jnp.float32) + total).astype(jnp.bfloat16)
            mixed[c] = (own_weight * block.astype(jnp.float32) + past[c]).astype(jnp.bfloat16)
            out_copy(c).start()
        if i == 1:
            with jax.named_scope("relay4"):
                relay(4)

    for way in range(2):
        settle(rows_all.at[me], ag_s.at[way], ag_r.at[way, 0]).wait_send()
        half_block = rows_all.at[me, :, pl.ds(0, width // 2)]
        settle(half_block, fw_s.at[way], fw_r.at[way, 0]).wait_send()

    for d in (0, *steps):

        @pl.when(cross_sent(d))
        def _():
            settle(cross_in.at[d], cross_s.at[d], cross_r.at[d, 0]).wait_send()

    for d in steps:

        @pl.when(onward(d))
        def _():
            settle(part_out.at[d - 1], part_s.at[d - 1], part_r.at[d - 1, 0]).wait_send()
            for which, raw in ((0, raw_a), (1, raw_b)):
                settle(raw.at[d - 1], raw_s.at[which, d - 1], raw_r.at[which, d - 1]).wait_send()

    @pl.when(pair_sent)
    def _():
        settle(pair_out, pair_s, pair_r.at[0]).wait_send()

    settle(far_send, far_s, far_r.at[0]).wait_send()
    settle(near_send, near_s, near_r.at[0, 0]).wait_send()
    with jax.named_scope("s_drain"):
        settle(mixed, out_s, out_r).wait_send()
        settle(out_hbm.at[0], out_s, out_r).wait_recv()


def solution(mesh):
    sections, tensor = mesh.shape["section"], mesh.shape["tensor"]
    assert tensor == 4 and sections == 32
    col_chunks = 8

    def on_device(x, history, wq, wk, wv, wo, mix_weights):
        rows, width = x.shape[1:]
        q_width, kv_width = wq.shape[2], wk.shape[2]
        seq = rows * tensor
        tile = 2 * kv_width
        q_tiles = q_width // tile
        cols = width // col_chunks
        summed, plain = len(SUMMED), len(PLAIN)
        bf16 = jnp.bfloat16
        dma = pltpu.SemaphoreType.DMA
        hbm = pl.BlockSpec(memory_space=pl.ANY)
        return pl.pallas_call(
            functools.partial(tick_kernel, sections),
            out_shape=jax.ShapeDtypeStruct(x.shape, bf16),
            in_specs=[hbm] * 7,
            out_specs=hbm,
            scratch_shapes=[
                pltpu.VMEM((rows, width), bf16),
                pltpu.VMEM((tensor, rows, width), bf16),
                pltpu.VMEM((q_tiles + 1, width, tile), bf16),
                pltpu.VMEM((col_chunks, q_width, cols), bf16),
                pltpu.VMEM((2 * q_tiles, seq, kv_width), bf16),
                pltpu.VMEM((4, seq, kv_width), bf16),
                pltpu.VMEM((4, seq, 2 * kv_width), bf16),
                pltpu.VMEM((tensor, rows, q_width), bf16),
                pltpu.VMEM((col_chunks, rows, cols), bf16),
                pltpu.VMEM((col_chunks, rows, cols), bf16),
                pltpu.VMEM((2, col_chunks, rows, cols), bf16),
                pltpu.VMEM((2, col_chunks, rows, cols), bf16),
                pltpu.VMEM((col_chunks, rows, cols), bf16),
                pltpu.VMEM((col_chunks, rows, cols), bf16),
                pltpu.VMEM((3, rows, width), bf16),
                pltpu.VMEM((4, summed, rows, cols), bf16),
                pltpu.VMEM((3, summed, rows, cols), bf16),
                pltpu.VMEM((3, summed, rows, cols), bf16),
                pltpu.VMEM((3, plain, rows, cols), bf16),
                pltpu.VMEM((3, plain, rows, cols), bf16),
                pltpu.VMEM((rows, width), bf16),
                pltpu.VMEM((plain, rows, cols), bf16),
                pltpu.VMEM((plain, rows, cols), bf16),
                pltpu.VMEM((col_chunks, rows, cols), jnp.float32),
                pltpu.VMEM(mix_weights.shape[::-1], mix_weights.dtype),
                dma((q_tiles + 2,)),
                dma((col_chunks,)),
                dma((PIECES,)),
                dma,
                dma((3,)),
                dma,
                dma((4,)),
                dma((4, summed)),
                dma((3,)),
                dma((3, summed)),
                dma((2, 3)),
                dma((2, 3)),
                dma,
                dma((plain,)),
                dma((2,)),
                dma((2, PIECES)),
                dma((2,)),
                dma((2, PIECES)),
                dma,
                dma((col_chunks,)),
                dma,
                dma((2, col_chunks)),
                dma,
                dma,
            ],
            compiler_params=pltpu.CompilerParams(
                collective_id=0, has_side_effects=True, vmem_limit_bytes=60 * 1024 * 1024
            ),
        )(x, history, wq, wk, wv, wo, mix_weights.T)

    placed = (
        P("section", "tensor", None),
        P("section", None, "tensor", None),
        P("section", None, "tensor"),
        P("section", None, "tensor"),
        P("section", None, "tensor"),
        P("section", "tensor", None),
        P(),
    )
    return jax.shard_map(
        on_device,
        mesh=mesh,
        in_specs=placed,
        out_specs=P("section", "tensor", None),
        check_vma=False,
    )
```

time: 92.7 us -> 85.6 us (0.923)
  the two profiles are of different devices: /device:TPU:2 before, /device:TPU:10 now
where the time goes in v3:
time: 85.6 us; the launch traced here: 85.5 us
  Pallas kernels  83.2 us (97%)
  local copies, waits for them, and re-layouts  2.29 us (3%)
    pallas_call x1, Pallas kernels, on_device(): pl.pallas_call(functools.partial(tick_kernel, sections), out_shape=jax.Sh...  83.2 us
    unnamed x1, local copies, waits for them, and re-layouts  2.29 us

profile of v3, /device:TPU:10, one launch (start us, length us, event | category | flops | bytes accessed | tf_op | source)
XLA Modules:
  0.0 85.5 jit_solution(1930861998648317350)
XLA Ops:
  0.0 83.2 %shard_map.73 = bf16[1,128,4096]{2,1,0:T(8,128)(2,1)} custom-call(bf16[1,128,4096]{2,1,0:T(8,128)(2,1)} %x_hbm.1, bf16[1,7,128,4096]{3,2,1,0:T(8,128)(2,1)} %hist_hbm.1, bf16[1,4096,768]{2,1,0:T(8,128)(2,1)} %wq_hbm.1, bf16[1,4096,128]{2,1,0:T(8,128)(2,1)} %wk_hbm.1, bf16[1,4096,128]{2,1,0:T(8,128)(2,1)} %wv_hbm.1, bf16[1,768,4096]{2,1,0:T(8,128)(2,1)} %wo_hbm.1, ...), custom_call_target="tpu_custom_call" | custom-call | tf_op jit(solution)/shard_map/pallas_call | solution.py:678
  83.2 2.3 %copy.9 = bf16[1,128,4096]{2,1,0:T(8,128)(2,1)} copy(bf16[1,128,4096]{2,1,0:T(8,128)(2,1)} %shard_map.73) | data formatting | bytes 2097152

commit v4 on v3

--- a/solution.py
+++ b/solution.py
@@ -161,7 +161,7 @@
             src_ref=place,
             dst_ref=place,
             send_sem=fw_s.at[way],
-            recv_sem=fw_r.at[way, p],
+            recv_sem=fw_r.at[p // 2],
             device_id={"tensor": to[way]},
             device_id_type=MESH,
         )
@@ -220,7 +220,7 @@
             hist_hbm.at[0, jnp.maximum(2 * d - 2 * col, 0), :, chunk(SUMMED[j])],
             cross_in.at[d, j],
             cross_s.at[d],
-            cross_r.at[d, j],
+            cross_r.at[0 if d else 1, j],
             partner,
         )
 
@@ -229,7 +229,7 @@
             part_out.at[d - 1, j],
             part_in.at[d - 1, j],
             part_s.at[d - 1],
-            part_r.at[d - 1, j],
+            part_r.at[j],
             others[d - 1],
         )
 
@@ -322,6 +322,12 @@
         return jnp.sum(jnp.where(at, table, 0.0), keepdims=True)
 
     def relay(j):
+        for count in steps:
+
+            @pl.when(row == 3 - count)
+            def _():
+                settle(cross_in.at[pl.ds(1, count), j], cross_s.at[1], cross_r.at[0, j]).wait_recv()
+
         for d in steps:
 
             @pl.when(onward(d))
@@ -330,7 +336,6 @@
                 partner_weight = weight(section + 8 * d, 2 * d - 1 + 2 * col)
                 if j == 0:
                     even_load(d).wait()
-                cross_copy(d, j).wait_recv()
                 value = own_weight * even[d - 1, :, chunk(SUMMED[j])].astype(jnp.float32)
                 value = value + partner_weight * cross_in[d, j].astype(jnp.float32)
                 part_out[d - 1, j] = value.astype(jnp.bfloat16)
@@ -366,11 +371,11 @@
             def _():
                 cross_copy(0, j).wait_recv()
 
-            for d in steps:
-
-                @pl.when(inward(d))
+            for count in steps:
+
+                @pl.when(row == count)
                 def _():
-                    part_copy(d, j).wait_recv()
+                    settle(part_in.at[pl.ds(0, count), j], part_s.at[0], part_r.at[j]).wait_recv()
 
             value = weight(section, 1) * cross_in[0, j].astype(jnp.float32)
             for d in steps:
@@ -506,7 +511,7 @@
             src_ref=near_send.at[way, c],
             dst_ref=final_in.at[way, c],
             send_sem=near_s,
-            recv_sem=near_r.at[way, c],
+            recv_sem=near_r.at[c],
             device_id={"tensor": to[way]},
             device_id_type=MESH,
         )
@@ -553,9 +558,7 @@
     attend(me, far > me, 0, rows)
 
     for h in range(2):
-        for p in (2 * h, 2 * h + 1):
-            for way in range(2):
-                passed(way, p, far).wait_recv()
+        settle(rows_all.at[far, pl.ds(h * short, short)], fw_s.at[0], fw_r.at[h]).wait_recv()
         with jax.named_scope(f"i_proj_far{h}"):
             project(((far, h * short, short),))
         with jax.named_scope(f"j_att_far{h}"):
@@ -619,8 +622,8 @@
             gather_past(c)
         with jax.named_scope(f"final{i}"):
             total = own_part[c].astype(jnp.float32)
+            settle(final_in.at[:, c], near_s, near_r.at[c]).wait_recv()
             for way in range(2):
-                near_copy(way, c).wait_recv()
                 total = total + final_in[way, c].astype(jnp.float32)
             block = (x_own[:, chunk(c)].astype(jnp.float32) + total).astype(jnp.bfloat16)
             mixed[c] = (own_weight * block.astype(jnp.float32) + past[c]).astype(jnp.bfloat16)
@@ -632,19 +635,19 @@
     for way in range(2):
         settle(rows_all.at[me], ag_s.at[way], ag_r.at[way, 0]).wait_send()
         half_block = rows_all.at[me, :, pl.ds(0, width // 2)]
-        settle(half_block, fw_s.at[way], fw_r.at[way, 0]).wait_send()
+        settle(half_block, fw_s.at[way], fw_r.at[0]).wait_send()
 
     for d in (0, *steps):
 
         @pl.when(cross_sent(d))
         def _():
-            settle(cross_in.at[d], cross_s.at[d], cross_r.at[d, 0]).wait_send()
+            settle(cross_in.at[d], cross_s.at[d], cross_r.at[0, 0]).wait_send()
 
     for d in steps:
 
         @pl.when(onward(d))
         def _():
-            settle(part_out.at[d - 1], part_s.at[d - 1], part_r.at[d - 1, 0]).wait_send()
+            settle(part_out.at[d - 1], part_s.at[d - 1], part_r.at[0]).wait_send()
             for which, raw in ((0, raw_a), (1, raw_b)):
                 settle(raw.at[d - 1], raw_s.at[which, d - 1], raw_r.at[which, d - 1]).wait_send()
 
@@ -653,7 +656,7 @@
         settle(pair_out, pair_s, pair_r.at[0]).wait_send()
 
     settle(far_send, far_s, far_r.at[0]).wait_send()
-    settle(near_send, near_s, near_r.at[0, 0]).wait_send()
+    settle(near_send, near_s, near_r.at[0]).wait_send()
     with jax.named_scope("s_drain"):
         settle(mixed, out_s, out_r).wait_send()
         settle(out_hbm.at[0], out_s, out_r).wait_recv()
@@ -677,7 +680,7 @@
         hbm = pl.BlockSpec(memory_space=pl.ANY)
         return pl.pallas_call(
             functools.partial(tick_kernel, sections),
-            out_shape=jax.ShapeDtypeStruct(x.shape, bf16),
+            out_shape=pltpu.VMEM(x.shape, bf16),
             in_specs=[hbm] * 7,
             out_specs=hbm,
             scratch_shapes=[
@@ -713,9 +716,9 @@
                 dma((3,)),
                 dma,
                 dma((4,)),
-                dma((4, summed)),
+                dma((2, summed)),
                 dma((3,)),
-                dma((3, summed)),
+                dma((summed,)),
                 dma((2, 3)),
                 dma((2, 3)),
                 dma,
@@ -723,11 +726,11 @@
                 dma((2,)),
                 dma((2, PIECES)),
                 dma((2,)),
-                dma((2, PIECES)),
+                dma((2,)),
                 dma,
                 dma((col_chunks,)),
                 dma,
-                dma((2, col_chunks)),
+                dma((col_chunks,)),
                 dma,
                 dma,
             ],

time: 85.6 us -> 83.9 us (0.980)
  local copies, waits for them, and re-layouts: 2.29 us -> 0.97 us
    unnamed x1, local copies, waits for them, and re-layouts: 2.29 us -> 0.97 us
where the time goes in v4:
time: 83.9 us; the launch traced here: 83.8 us
  Pallas kernels  82.8 us (99%)
  local copies, waits for them, and re-layouts  0.97 us (1%)
    pallas_call x1, Pallas kernels, on_device(): pl.pallas_call(functools.partial(tick_kernel, sections), out_shape=pltpu....  82.8 us

profile of v4, /device:TPU:10, one launch (start us, length us, event | category | flops | bytes accessed | tf_op | source)
XLA Modules:
  0.0 83.8 jit_solution(8589551499599749072)
XLA Ops:
  0.0 82.8 %shard_map.73 = bf16[1,128,4096]{2,1,0:T(8,128)(2,1)S(1)} custom-call(bf16[1,128,4096]{2,1,0:T(8,128)(2,1)} %x_hbm.1, bf16[1,7,128,4096]{3,2,1,0:T(8,128)(2,1)} %hist_hbm.1, bf16[1,4096,768]{2,1,0:T(8,128)(2,1)} %wq_hbm.1, bf16[1,4096,128]{2,1,0:T(8,128)(2,1)} %wk_hbm.1, bf16[1,4096,128]{2,1,0:T(8,128)(2,1)} %wv_hbm.1, bf16[1,768,4096]{2,1,0:T(8,128)(2,1)} %wo_hbm.1, ...), custom_call_target="tpu_custom_call" | custom-call | tf_op jit(solution)/shard_map/pallas_call | solution.py:681
  82.8 1.0 %copy.9 = bf16[1,128,4096]{2,1,0:T(8,128)(2,1)} copy(bf16[1,128,4096]{2,1,0:T(8,128)(2,1)S(1)} %shard_map.73) | data formatting | bytes 2097152

commit v5 on v4

--- a/solution.py
+++ b/solution.py
@@ -9,8 +9,9 @@
 from jax.sharding import PartitionSpec as P
 
 HEAD_DIM = 64
-SUMMED = (4, 0, 5, 1, 3)
-PLAIN = (6, 2, 7)
+ORDER = (4, 0, 5, 1, 6, 2, 7, 3)
+SUMMED = {1: range(0, 3), 2: range(0, 8), 3: range(6, 8)}
+PLAIN = {1: range(3, 8), 3: range(0, 6)}
 MESH = pl.DeviceIdType.MESH
 PIECES = 4
 
@@ -199,12 +200,6 @@
     def inward(d):
         return row >= d
 
-    def cross_sent(d):
-        return onward(d) if d else col == 0
-
-    def cross_due(d):
-        return onward(d) if d else col == 1
-
     def section_copy(src, dst, send, recv, target):
         return pltpu.make_async_remote_copy(
             src_ref=src,
@@ -215,36 +210,43 @@
             device_id_type=MESH,
         )
 
-    def cross_copy(d, j):
+    def cross_copy(d, i):
         return section_copy(
-            hist_hbm.at[0, jnp.maximum(2 * d - 2 * col, 0), :, chunk(SUMMED[j])],
-            cross_in.at[d, j],
-            cross_s.at[d],
-            cross_r.at[0 if d else 1, j],
+            hist_hbm.at[0, jnp.maximum(2 * d - 2 * col, 0), :, chunk(ORDER[i])],
+            cross_in.at[d - 1, i],
+            cross_s.at[d - 1],
+            cross_r.at[d - 1, i],
             partner,
         )
 
-    def part_copy(d, j):
+    def part_copy(d, i):
         return section_copy(
-            part_out.at[d - 1, j],
-            part_in.at[d - 1, j],
+            part_out.at[d - 1, i],
+            part_in.at[d - 1, i],
             part_s.at[d - 1],
-            part_r.at[j],
+            part_r.at[d - 1, i],
             others[d - 1],
         )
 
-    def raw_copy(d, which, n):
+    def raw_copy(d, which, i):
         slot = 2 * d - 1 if which == 0 else 2 * d - 2 * col
         return section_copy(
-            hist_hbm.at[0, slot, :, chunk(PLAIN[n])],
-            (raw_a, raw_b)[which].at[d - 1, n],
+            hist_hbm.at[0, slot, :, chunk(ORDER[i])],
+            (raw_a, raw_b)[which].at[d - 1, i],
             raw_s.at[which, d - 1],
-            raw_r.at[which, d - 1],
+            raw_r.at[d - 1, i if which == 0 else col_chunks],
             others[d - 1],
         )
 
-    def pair_copy(n):
-        return section_copy(pair_out.at[n], pair_in.at[n], pair_s, pair_r.at[n], partner)
+    def plain(d):
+        return pl.ds(PLAIN[d].start, len(PLAIN[d]))
+
+    def raw_wait(d, which):
+        raw = (raw_a, raw_b)[which].at[d - 1, plain(d)]
+        return settle(raw, raw_s.at[which, d - 1], raw_r.at[d - 1, col_chunks])
+
+    def pair_copy(i):
+        return section_copy(pair_out.at[i], pair_in.at[i], pair_s, pair_r.at[i], partner)
 
     pair_sent = (row >= 1) | (col == 0)
     pair_due = (row >= 1) | (col == 1)
@@ -256,23 +258,21 @@
 
     first_load = pltpu.make_async_copy(hist_hbm.at[0, 0], first, first_sem)
 
-    def cross(some):
-        for j in some:
-            for d in (1, 2, 3, 0):
-
-                @pl.when(cross_sent(d))
+    for i in range(col_chunks):
+        for d in steps:
+            if i in SUMMED[d]:
+
+                @pl.when(onward(d))
                 def _():
-                    cross_copy(d, j).start()
-
-    cross(range(len(SUMMED)))
+                    cross_copy(d, i).start()
 
     for which in (1, 0):
-        for d in steps:
+        for d in (1, 3):
 
             @pl.when(onward(d))
             def _():
-                for n in range(len(PLAIN)):
-                    raw_copy(d, which, n).start()
+                for i in PLAIN[d]:
+                    raw_copy(d, which, i).start()
 
     out_loads = []
     for c in range(col_chunks):
@@ -292,14 +292,16 @@
 
         @pl.when(row < d)
         def _():
-            part_in[d - 1] = jnp.zeros(part_in.shape[1:], part_in.dtype)
-            raw_a[d - 1] = jnp.zeros(raw_a.shape[1:], raw_a.dtype)
-            raw_b[d - 1] = jnp.zeros(raw_b.shape[1:], raw_b.dtype)
+            for i in range(col_chunks):
+                if i in SUMMED[d]:
+                    part_in[d - 1, i] = jnp.zeros((rows, cols), part_in.dtype)
+                else:
+                    raw_a[d - 1, i] = jnp.zeros((rows, cols), raw_a.dtype)
+                    raw_b[d - 1, i] = jnp.zeros((rows, cols), raw_b.dtype)
 
     @pl.when(col == 0)
     def _():
         first_load.start()
-        cross_in[0] = jnp.zeros(cross_in.shape[1:], cross_in.dtype)
 
     @pl.when(col == 1)
     def _():
@@ -321,83 +323,67 @@
         )
         return jnp.sum(jnp.where(at, table, 0.0), keepdims=True)
 
-    def relay(j):
-        for count in steps:
-
-            @pl.when(row == 3 - count)
-            def _():
-                settle(cross_in.at[pl.ds(1, count), j], cross_s.at[1], cross_r.at[0, j]).wait_recv()
-
+    def relay(some):
         for d in steps:
 
             @pl.when(onward(d))
             def _():
                 own_weight = weight(section + 8 * d, 2 * d)
                 partner_weight = weight(section + 8 * d, 2 * d - 1 + 2 * col)
-                if j == 0:
+                if 0 in some:
                     even_load(d).wait()
-                value = own_weight * even[d - 1, :, chunk(SUMMED[j])].astype(jnp.float32)
-                value = value + partner_weight * cross_in[d, j].astype(jnp.float32)
-                part_out[d - 1, j] = value.astype(jnp.bfloat16)
-                part_copy(d, j).start()
-
-    def relay_pair():
-        @pl.when(col == 0)
+                for i in some:
+                    if i in SUMMED[d]:
+                        cross_copy(d, i).wait_recv()
+                        value = own_weight * even[d - 1, :, chunk(ORDER[i])].astype(jnp.float32)
+                        value = value + partner_weight * cross_in[d - 1, i].astype(jnp.float32)
+                        part_out[d - 1, i] = value.astype(jnp.bfloat16)
+                        part_copy(d, i).start()
+
+    def relay_pair(some):
+        if 0 in some:
+
+            @pl.when(col == 0)
+            def _():
+                first_load.wait()
+
+            for d in (1, 3):
+
+                @pl.when(inward(d))
+                def _():
+                    raw_wait(d, 1).wait_recv()
+
+        @pl.when(pair_sent)
         def _():
-            first_load.wait()
+            weights = {d: weight(partner, 2 * d + 1 - 2 * col) for d in (1, 3)}
+            first_weight = weight(partner, 1)
+            for i in some:
+                value = first_weight * first[:, chunk(ORDER[i])].astype(jnp.float32)
+                for d in (1, 3):
+                    if i not in SUMMED[d]:
+                        value = value + weights[d] * raw_b[d - 1, i].astype(jnp.float32)
+                pair_out[i] = value.astype(jnp.bfloat16)
+                pair_copy(i).start()
+
+    def gather_past(i):
+        @pl.when(pair_due)
+        def _():
+            pair_copy(i).wait_recv()
 
         for d in steps:
+            arriving = part_copy(d, i) if i in SUMMED[d] else raw_copy(d, 0, i)
 
             @pl.when(inward(d))
             def _():
-                settle(raw_b.at[d - 1], raw_s.at[1, d - 1], raw_r.at[1, d - 1]).wait_recv()
-
-        @pl.when(pair_sent)
-        def _():
-            weights = [weight(partner, 2 * d + 1 - 2 * col) for d in steps]
-            first_weight = weight(partner, 1)
-            for n, c in enumerate(PLAIN):
-                value = first_weight * first[:, chunk(c)].astype(jnp.float32)
-                for d in steps:
-                    value = value + weights[d - 1] * raw_b[d - 1, n].astype(jnp.float32)
-                pair_out[n] = value.astype(jnp.bfloat16)
-                pair_copy(n).start()
-
-    def gather_past(c):
-        if c in SUMMED:
-            j = SUMMED.index(c)
-
-            @pl.when(col == 1)
-            def _():
-                cross_copy(0, j).wait_recv()
-
-            for count in steps:
-
-                @pl.when(row == count)
-                def _():
-                    settle(part_in.at[pl.ds(0, count), j], part_s.at[0], part_r.at[j]).wait_recv()
-
-            value = weight(section, 1) * cross_in[0, j].astype(jnp.float32)
-            for d in steps:
-                value = value + part_in[d - 1, j].astype(jnp.float32)
-        else:
-            n = PLAIN.index(c)
-
-            @pl.when(pair_due)
-            def _():
-                pair_copy(n).wait_recv()
-
-            if n == 0:
-                for d in steps:
-
-                    @pl.when(inward(d))
-                    def _():
-                        settle(raw_a.at[d - 1], raw_s.at[0, d - 1], raw_r.at[0, d - 1]).wait_recv()
-
-            value = pair_in[n].astype(jnp.float32)
-            for d in steps:
-                value = value + weight(section, 2 * d) * raw_a[d - 1, n].astype(jnp.float32)
-        past[c] = value
+                arriving.wait_recv()
+
+        value = pair_in[i].astype(jnp.float32)
+        for d in steps:
+            if i in SUMMED[d]:
+                value = value + part_in[d - 1, i].astype(jnp.float32)
+            else:
+                value = value + weight(section, 2 * d) * raw_a[d - 1, i].astype(jnp.float32)
+        past[ORDER[i]] = value
 
     scale = 1.0 / math.sqrt(HEAD_DIM)
 
@@ -548,9 +534,9 @@
         if p == 1:
             load_mix.wait()
             with jax.named_scope("relay0"):
-                relay(0)
+                relay((0,))
     with jax.named_scope("relay1"):
-        relay(1)
+        relay((1,))
     for copy in out_loads:
         copy.wait()
     with jax.named_scope("f_proj_near"):
@@ -576,14 +562,15 @@
             lax.fori_loop(0, side, far_step, 0)
         if h == 0:
             with jax.named_scope("relay2"):
-                relay(2)
+                relay((2, 3, 4))
             with jax.named_scope("relay_pair"):
-                relay_pair()
+                relay_pair((0, 1, 2, 3))
 
     attend(right, True, 0, rows)
     attend(left, True, 0, rows)
     with jax.named_scope("relay3"):
-        relay(3)
+        relay((5, 6, 7))
+        relay_pair((4, 5, 6, 7))
 
     def near_step(i, carry):
         def relayed(way):
@@ -617,9 +604,9 @@
     own_weight = weight(section, 0)
 
     for i in range(col_chunks):
-        c = (i + 1) % 2 * side + i // 2
+        c = ORDER[i]
         with jax.named_scope(f"past{i}"):
-            gather_past(c)
+            gather_past(i)
         with jax.named_scope(f"final{i}"):
             total = own_part[c].astype(jnp.float32)
             settle(final_in.at[:, c], near_s, near_r.at[c]).wait_recv()
@@ -628,28 +615,21 @@
             block = (x_own[:, chunk(c)].astype(jnp.float32) + total).astype(jnp.bfloat16)
             mixed[c] = (own_weight * block.astype(jnp.float32) + past[c]).astype(jnp.bfloat16)
             out_copy(c).start()
-        if i == 1:
-            with jax.named_scope("relay4"):
-                relay(4)
-
     for way in range(2):
         settle(rows_all.at[me], ag_s.at[way], ag_r.at[way, 0]).wait_send()
         half_block = rows_all.at[me, :, pl.ds(0, width // 2)]
         settle(half_block, fw_s.at[way], fw_r.at[0]).wait_send()
 
-    for d in (0, *steps):
-
-        @pl.when(cross_sent(d))
-        def _():
-            settle(cross_in.at[d], cross_s.at[d], cross_r.at[0, 0]).wait_send()
-
     for d in steps:
 
         @pl.when(onward(d))
         def _():
-            settle(part_out.at[d - 1], part_s.at[d - 1], part_r.at[0]).wait_send()
-            for which, raw in ((0, raw_a), (1, raw_b)):
-                settle(raw.at[d - 1], raw_s.at[which, d - 1], raw_r.at[which, d - 1]).wait_send()
+            sent = pl.ds(SUMMED[d].start, len(SUMMED[d]))
+            settle(cross_in.at[d - 1, sent], cross_s.at[d - 1], cross_r.at[0, 0]).wait_send()
+            settle(part_out.at[d - 1, sent], part_s.at[d - 1], part_r.at[0, 0]).wait_send()
+            if d in PLAIN:
+                raw_wait(d, 0).wait_send()
+                raw_wait(d, 1).wait_send()
 
     @pl.when(pair_sent)
     def _():
@@ -674,7 +654,6 @@
         tile = 2 * kv_width
         q_tiles = q_width // tile
         cols = width // col_chunks
-        summed, plain = len(SUMMED), len(PLAIN)
         bf16 = jnp.bfloat16
         dma = pltpu.SemaphoreType.DMA
         hbm = pl.BlockSpec(memory_space=pl.ANY)
@@ -699,14 +678,14 @@
                 pltpu.VMEM((col_chunks, rows, cols), bf16),
                 pltpu.VMEM((col_chunks, rows, cols), bf16),
                 pltpu.VMEM((3, rows, width), bf16),
-                pltpu.VMEM((4, summed, rows, cols), bf16),
-                pltpu.VMEM((3, summed, rows, cols), bf16),
-                pltpu.VMEM((3, summed, rows, cols), bf16),
-                pltpu.VMEM((3, plain, rows, cols), bf16),
-                pltpu.VMEM((3, plain, rows, cols), bf16),
+                pltpu.VMEM((3, col_chunks, rows, cols), bf16),
+                pltpu.VMEM((3, col_chunks, rows, cols), bf16),
+                pltpu.VMEM((3, col_chunks, rows, cols), bf16),
+                pltpu.VMEM((3, col_chunks, rows, cols), bf16),
+                pltpu.VMEM((3, col_chunks, rows, cols), bf16),
                 pltpu.VMEM((rows, width), bf16),
-                pltpu.VMEM((plain, rows, cols), bf16),
-                pltpu.VMEM((plain, rows, cols), bf16),
+                pltpu.VMEM((col_chunks, rows, cols), bf16),
+                pltpu.VMEM((col_chunks, rows, cols), bf16),
                 pltpu.VMEM((col_chunks, rows, cols), jnp.float32),
                 pltpu.VMEM(mix_weights.shape[::-1], mix_weights.dtype),
                 dma((q_tiles + 2,)),
@@ -715,14 +694,14 @@
                 dma,
                 dma((3,)),
                 dma,
-                dma((4,)),
-                dma((2, summed)),
                 dma((3,)),
-                dma((summed,)),
+                dma((3, col_chunks)),
+                dma((3,)),
+                dma((3, col_chunks)),
                 dma((2, 3)),
-                dma((2, 3)),
+                dma((3, col_chunks + 1)),
                 dma,
-                dma((plain,)),
+                dma((col_chunks,)),
                 dma((2,)),
                 dma((2, PIECES)),
                 dma((2,)),

time: 83.9 us -> 81.9 us (0.976)
  Pallas kernels: 82.8 us -> 80.3 us
    pallas_call x1, Pallas kernels: 82.8 us -> 80.3 us  [on_device(): pl.pallas_call(functools.partial(tick_kernel, sections), out_shape=pltpu....]
where the time goes in v5:
time: 81.9 us; the launch traced here: 81.3 us
  Pallas kernels  80.3 us (98%)
  local copies, waits for them, and re-layouts  0.97 us (1%)
    pallas_call x1, Pallas kernels, on_device(): pl.pallas_call(functools.partial(tick_kernel, sections), out_shape=pltpu....  80.3 us

profile of v5, /device:TPU:10, one launch (start us, length us, event | category | flops | bytes accessed | tf_op | source)
XLA Modules:
  0.0 81.3 jit_solution(17897521285256544236)
XLA Ops:
  0.0 80.3 %shard_map.73 = bf16[1,128,4096]{2,1,0:T(8,128)(2,1)S(1)} custom-call(bf16[1,128,4096]{2,1,0:T(8,128)(2,1)} %x_hbm.1, bf16[1,7,128,4096]{3,2,1,0:T(8,128)(2,1)} %hist_hbm.1, bf16[1,4096,768]{2,1,0:T(8,128)(2,1)} %wq_hbm.1, bf16[1,4096,128]{2,1,0:T(8,128)(2,1)} %wk_hbm.1, bf16[1,4096,128]{2,1,0:T(8,128)(2,1)} %wv_hbm.1, bf16[1,768,4096]{2,1,0:T(8,128)(2,1)} %wo_hbm.1, ...), custom_call_target="tpu_custom_call" | custom-call | tf_op jit(solution)/shard_map/pallas_call | solution.py:660
  80.3 1.0 %copy.9 = bf16[1,128,4096]{2,1,0:T(8,128)(2,1)} copy(bf16[1,128,4096]{2,1,0:T(8,128)(2,1)S(1)} %shard_map.73) | data formatting | bytes 2097152

commit v6 on v5

--- a/solution.py
+++ b/solution.py
@@ -12,6 +12,8 @@
 ORDER = (4, 0, 5, 1, 6, 2, 7, 3)
 SUMMED = {1: range(0, 3), 2: range(0, 8), 3: range(6, 8)}
 PLAIN = {1: range(3, 8), 3: range(0, 6)}
+SUMMED_AT = {1: 0, 2: 3, 3: 5}
+PLAIN_AT = {1: -3, 3: 5}
 MESH = pl.DeviceIdType.MESH
 PIECES = 4
 
@@ -182,12 +184,8 @@
 
     norm_piece(0)
     pl.semaphore_wait(barrier, 8)
-    for p in range(PIECES):
-        if p:
-            load_x(p).wait()
-            norm_piece(p)
-        own_copy(0, p).start()
-        own_copy(1, p).start()
+    own_copy(0, 0).start()
+    own_copy(1, 0).start()
 
     steps = range(1, 4)
 
@@ -215,7 +213,7 @@
             hist_hbm.at[0, jnp.maximum(2 * d - 2 * col, 0), :, chunk(ORDER[i])],
             cross_in.at[d - 1, i],
             cross_s.at[d - 1],
-            cross_r.at[d - 1, i],
+            cross_r.at[SUMMED_AT[d] + i],
             partner,
         )
 
@@ -224,7 +222,7 @@
             part_out.at[d - 1, i],
             part_in.at[d - 1, i],
             part_s.at[d - 1],
-            part_r.at[d - 1, i],
+            part_r.at[SUMMED_AT[d] + i],
             others[d - 1],
         )
 
@@ -234,7 +232,7 @@
             hist_hbm.at[0, slot, :, chunk(ORDER[i])],
             (raw_a, raw_b)[which].at[d - 1, i],
             raw_s.at[which, d - 1],
-            raw_r.at[d - 1, i if which == 0 else col_chunks],
+            raw_r.at[PLAIN_AT[d] + i if which == 0 else 11 + d // 2],
             others[d - 1],
         )
 
@@ -243,7 +241,7 @@
 
     def raw_wait(d, which):
         raw = (raw_a, raw_b)[which].at[d - 1, plain(d)]
-        return settle(raw, raw_s.at[which, d - 1], raw_r.at[d - 1, col_chunks])
+        return settle(raw, raw_s.at[which, d - 1], raw_r.at[11 + d // 2])
 
     def pair_copy(i):
         return section_copy(pair_out.at[i], pair_in.at[i], pair_s, pair_r.at[i], partner)
@@ -273,6 +271,12 @@
             def _():
                 for i in PLAIN[d]:
                     raw_copy(d, which, i).start()
+
+    for p in range(1, PIECES):
+        load_x(p).wait()
+        norm_piece(p)
+        own_copy(0, p).start()
+        own_copy(1, p).start()
 
     out_loads = []
     for c in range(col_chunks):
@@ -625,8 +629,8 @@
         @pl.when(onward(d))
         def _():
             sent = pl.ds(SUMMED[d].start, len(SUMMED[d]))
-            settle(cross_in.at[d - 1, sent], cross_s.at[d - 1], cross_r.at[0, 0]).wait_send()
-            settle(part_out.at[d - 1, sent], part_s.at[d - 1], part_r.at[0, 0]).wait_send()
+            settle(cross_in.at[d - 1, sent], cross_s.at[d - 1], cross_r.at[0]).wait_send()
+            settle(part_out.at[d - 1, sent], part_s.at[d - 1], part_r.at[0]).wait_send()
             if d in PLAIN:
                 raw_wait(d, 0).wait_send()
                 raw_wait(d, 1).wait_send()
@@ -695,11 +699,11 @@
                 dma((3,)),
                 dma,
                 dma((3,)),
-                dma((3, col_chunks)),
+                dma((13,)),
                 dma((3,)),
-                dma((3, col_chunks)),
+                dma((13,)),
                 dma((2, 3)),
-                dma((3, col_chunks + 1)),
+                dma((13,)),
                 dma,
                 dma((col_chunks,)),
                 dma((2,)),

time: 81.9 us -> 81.6 us (level); the launches traced: 81.3 us -> 80 us
  Pallas kernels: 80.3 us -> 79 us
    pallas_call x1, Pallas kernels: 80.3 us -> 79 us  [on_device(): pl.pallas_call(functools.partial(tick_kernel, sections), out_shape=pltpu....]
where the time goes in v6:
time: 81.6 us; the launch traced here: 80 us
  Pallas kernels  79 us (97%)
  local copies, waits for them, and re-layouts  0.97 us (1%)
    pallas_call x1, Pallas kernels, on_device(): pl.pallas_call(functools.partial(tick_kernel, sections), out_shape=pltpu....  79 us

profile of v6, /device:TPU:10, one launch (start us, length us, event | category | flops | bytes accessed | tf_op | source)
XLA Modules:
  0.0 80.0 jit_solution(3522726780747107055)
XLA Ops:
  0.0 79.0 %shard_map.73 = bf16[1,128,4096]{2,1,0:T(8,128)(2,1)S(1)} custom-call(bf16[1,128,4096]{2,1,0:T(8,128)(2,1)} %x_hbm.1, bf16[1,7,128,4096]{3,2,1,0:T(8,128)(2,1)} %hist_hbm.1, bf16[1,4096,768]{2,1,0:T(8,128)(2,1)} %wq_hbm.1, bf16[1,4096,128]{2,1,0:T(8,128)(2,1)} %wk_hbm.1, bf16[1,4096,128]{2,1,0:T(8,128)(2,1)} %wv_hbm.1, bf16[1,768,4096]{2,1,0:T(8,128)(2,1)} %wo_hbm.1, ...), custom_call_target="tpu_custom_call" | custom-call | tf_op jit(solution)/shard_map/pallas_call | solution.py:664
  79.1 1.0 %copy.9 = bf16[1,128,4096]{2,1,0:T(8,128)(2,1)} copy(bf16[1,128,4096]{2,1,0:T(8,128)(2,1)S(1)} %shard_map.73) | data formatting | bytes 2097152
